TPU v7x, 16 devices: a whole 2x2x2 slice. The times are simulated.
16 devices in a mesh: shard: 2 (over z), worker: 8 (over y, x, core).
Axes of the slice: x: 2, y: 2, z: 2, core: 2. Of those that a mesh axis runs over, the one named last changes fastest.
Arguments:
- w1_local: float32 [16, 4, 256, 1024], P(('shard', 'worker'))
- w2_local: float32 [16, 4, 1024, 256], P(('shard', 'worker'))
- w1_global: float32 [4, 256, 1024], replicated
- w2_global: float32 [4, 1024, 256], replicated
- mom1: float32 [4, 256, 1024], replicated
- mom2: float32 [4, 1024, 256], replicated
- x_batches: bfloat16 [16, 4, 128, 256], P(('shard', 'worker'))
- y_targets: bfloat16 [16, 4, 128, 256], P(('shard', 'worker'))
Outputs:
- output 1: float32 [16, 4, 256, 1024], P(('shard', 'worker'))
- output 2: float32 [16, 4, 1024, 256], P(('shard', 'worker'))
- output 3: float32 [4, 256, 1024], replicated
- output 4: float32 [4, 1024, 256], replicated
- output 5: float32 [4, 256, 1024], replicated
- output 6: float32 [4, 1024, 256], replicated
All inputs are finite; a program needn't handle non-finite values.
Results may differ from a plain program's by a relative error of at most 0.00194075.
Values are sent between devices in bfloat16 or wider.
A program may use at most 1 GiB of HBM per device.

v0:
```python
import jax
import jax.numpy as jnp
from jax import lax
from jax.experimental import pallas as pl
from jax.experimental.pallas import tpu as pltpu
from jax.sharding import PartitionSpec as P

OUTER_LR = 0.7
OUTER_MOM = 0.9
MERGE_MIX = 0.5

L = 4
H = 4
D = 256
FF = 1024
B = 128
NB = FF // D
INNER_LR = 2.0 * D / (FF * L)
N_ALL = 16
F32 = jnp.float32
BF16 = jnp.bfloat16
MESH = pl.DeviceIdType.MESH
ANY = pl.BlockSpec(memory_space=pl.ANY)
VMEM = pl.BlockSpec(memory_space=pltpu.VMEM)

PIECES = ((1, 2), (1, 1), (0, 2), (0, 1))
COLOR_UNITS = ((3, 3, 2), (3, 2, 3), (2, 3, 3), (3, 3, 2))
GROUPS = []
for piece_idx in range(4):
    first_unit = 0
    for color in range(3):
        GROUPS.append((piece_idx, color, first_unit, COLOR_UNITS[piece_idx][color]))
        first_unit += COLOR_UNITS[piece_idx][color]
RS1, RS2, AG0, AG1, AG2, DDA, DDB = range(7)


def dot(a, b, ca, cb):
    return lax.dot_general(a, b, (((ca,), (cb,)), ((), ())), preferred_element_type=F32)


def gelu_pair(a):
    k0 = 0.7978845608028654
    a2 = a * a
    t = jnp.tanh(k0 * (a + 0.044715 * (a2 * a)))
    half = 0.5 * (1.0 + t)
    u = a * half
    du = half + (0.5 * a) * (1.0 - t * t) * (k0 * (1.0 + (3 * 0.044715) * a2))
    return u, du


def main_body(w1_in, w2_in, g1_in, g2_in, m1_in, m2_in, x_in, y_in,
              w1, w2, g1, g2, m1, m2,
              xb, yb, w1b, w2b, hb, ub, du, hid, dhid,
              delta, raw, s1, r1, s2, r2, full,
              ld_sem, s0_send, s0_recv, st_send, st_recv):
    zc = lax.axis_index('shard')
    wk = lax.axis_index('worker')
    core = lax.rem(wk, 2)
    xc = lax.rem(wk // 2, 2)
    yc = wk // 4
    coord = (xc, yc, zc)

    def chip_peer(dim, same_core=True):
        w = wk
        s = zc
        if dim == 0:
            w = wk + 2 - 4 * xc
        elif dim == 1:
            w = wk + 4 - 8 * yc
        elif dim == 2:
            s = 1 - zc
        if not same_core:
            w = w + 1 - 2 * core
        return (s, w)

    partner = chip_peer(3, False)

    bar = pltpu.get_barrier_semaphore()
    pl.semaphore_signal(bar, inc=1, device_id=partner, device_id_type=MESH)
    for dim in range(3):
        for same in (True, False):
            pl.semaphore_signal(bar, inc=1, device_id=chip_peer(dim, same), device_id_type=MESH)

    def loads():
        cps = [pltpu.make_async_copy(x_in.at[0], xb, ld_sem.at[24]),
               pltpu.make_async_copy(y_in.at[0], yb, ld_sem.at[25])]
        for lay in range(L):
            cps.append(pltpu.make_async_copy(w1_in.at[0, lay], w1.at[0, lay], ld_sem.at[lay]))
            cps.append(pltpu.make_async_copy(w2_in.at[0, lay], w2.at[0, lay], ld_sem.at[4 + lay]))
        gcps = []
        for lay in range(L):
            gcps.append(pltpu.make_async_copy(g1_in.at[lay], g1.at[lay], ld_sem.at[8 + lay]))
            gcps.append(pltpu.make_async_copy(g2_in.at[lay], g2.at[lay], ld_sem.at[12 + lay]))
            gcps.append(pltpu.make_async_copy(m1_in.at[lay], m1.at[lay], ld_sem.at[16 + lay]))
            gcps.append(pltpu.make_async_copy(m2_in.at[lay], m2.at[lay], ld_sem.at[20 + lay]))
        return cps, gcps

    cps, gcps = loads()
    for cp in cps + gcps:
        cp.start()
    cps[0].wait()
    cps[1].wait()
    for lay in range(L):
        cps[2 + 2 * lay].wait()
        cps[3 + 2 * lay].wait()

        def cast1(i, _, lay=lay):
            rows = pl.ds(pl.multiple_of(i * 32, 32), 32)
            w1b[lay, rows, :] = w1[0, lay, rows, :].astype(BF16)
            return 0

        def cast2(i, _, lay=lay):
            rows = pl.ds(pl.multiple_of(i * 128, 128), 128)
            w2b[lay, rows, :] = w2[0, lay, rows, :].astype(BF16)
            return 0

        lax.fori_loop(0, D // 32, cast1, 0)
        lax.fori_loop(0, FF // 128, cast2, 0)
    for cp in gcps:
        cp.wait()
    pl.semaphore_wait(bar, 7)

    def dims_of(color_idx):
        return color_idx % 3, (color_idx + 1) % 3, (color_idx + 2) % 3

    def rs0_copies(gi):
        p, c, u0, nu = GROUPS[gi]
        d0 = dims_of(c)[0]
        k0 = coord[d0]
        us = pl.ds(u0, nu)
        other = 1 - core

        def rows(tc, blk):
            return pl.ds(pl.multiple_of(tc * 64 + blk * 32, 32), 32)

        out = []
        for idx, (tc, blk, dev) in enumerate(((other, k0, partner),
                                               (core, 1 - k0, chip_peer(d0, True)),
                                               (other, 1 - k0, chip_peer(d0, False)))):
            out.append(pltpu.make_async_remote_copy(
                src_ref=delta.at[p, us, rows(tc, blk)], dst_ref=raw.at[idx, p, us],
                send_sem=s0_send.at[gi, idx], recv_sem=s0_recv.at[gi, idx],
                device_id=dev, device_id_type=MESH))
        return out

    def stage_copy(stage, gi):
        p, c, u0, nu = GROUPS[gi]
        d0, d1, d2 = dims_of(c)
        k0, k1, k2 = coord[d0], coord[d1], coord[d2]
        us = pl.ds(u0, nu)
        if stage == RS1:
            src, dst, dev = s1.at[p, us, pl.ds(pl.multiple_of((1 - k1) * 16, 16), 16)], r1.at[p, us], chip_peer(d1)
        elif stage == RS2:
            src, dst, dev = s2.at[p, us, pl.ds(pl.multiple_of((1 - k2) * 8, 8), 8)], r2.at[p, us], chip_peer(d2)
        else:
            base = core * 64
            if stage == AG0:
                off, n, dev = base + k0 * 32 + k1 * 16 + k2 * 8, 8, chip_peer(d2)
            elif stage == AG1:
                off, n, dev = base + k0 * 32 + k1 * 16, 16, chip_peer(d1)
            elif stage == AG2:
                off, n, dev = base + k0 * 32, 32, chip_peer(d0)
            elif stage == DDA:
                off, n, dev = base + k0 * 32, 32, partner
            else:
                off, n, dev = base + (1 - k0) * 32, 32, partner
            src = full.at[p, us, pl.ds(pl.multiple_of(off, 8), n)]
            dst = src
        return pltpu.make_async_remote_copy(
            src_ref=src, dst_ref=dst, send_sem=st_send.at[stage, gi], recv_sem=st_recv.at[stage, gi],
            device_id=dev, device_id_type=MESH)

    def unit_slice(mat, u):
        if mat == 2:
            return pl.ds(u * 128, 128), pl.ds(0, 256)
        return pl.ds((u % 2) * 128, 128), pl.ds((u // 2) * 256, 256)

    def make_delta(p, lay):
        mat = PIECES[p][1]
        wr, gr = (w1, g1) if mat == 1 else (w2, g2)
        for u in range(8):
            rows, cols = unit_slice(mat, u)
            delta[p, u] = (gr[lay, rows, cols] - wr[0, lay, rows, cols]).astype(BF16)
        for gi in range(3 * p, 3 * p + 3):
            for cp in rs0_copies(gi):
                cp.start()

    def forward(k):
        hid[...] = xb[k].astype(F32)

        def layer(lay, _):
            h_bf = hid[...].astype(BF16)
            hb[lay] = h_bf
            acc = hid[...]
            for j in range(NB):
                cols = slice(j * D, (j + 1) * D)
                a = dot(h_bf, w1b[lay, :, cols], 1, 0)
                u, dg = gelu_pair(a)
                u_bf = u.astype(BF16)
                ub[lay, :, cols] = u_bf
                du[lay, :, cols] = dg
                acc = acc + dot(u_bf, w2b[lay, cols, :], 1, 0)
            hid[...] = acc
            return 0

        lax.fori_loop(0, L, layer, 0)

    def backward(k):
        frag = k // 2
        dhid[...] = (2.0 / (B * D)) * (hid[...] - yb[k].astype(F32))

        def layer(li, _):
            lay = (L - 1) - li
            e = dhid[...].astype(BF16)
            h_bf = hb[lay]
            acc = dhid[...]
            for j in range(NB):
                cols = slice(j * D, (j + 1) * D)
                d_u = dot(e, w2b[lay, cols, :], 1, 1)
                c = (du[lay, :, cols] * d_u).astype(BF16)
                g_w2 = dot(ub[lay, :, cols], e, 0, 0)
                new2 = w2[0, lay, cols, :] - INNER_LR * g_w2
                w2[0, lay, cols, :] = new2
                w2b[lay, cols, :] = new2.astype(BF16)
                acc = acc + dot(c, w1b[lay, :, cols], 1, 1)
                g_w1 = dot(h_bf, c, 0, 0)
                new1 = w1[0, lay, :, cols] - INNER_LR * g_w1
                w1[0, lay, :, cols] = new1
                w1b[lay, :, cols] = new1.astype(BF16)
            dhid[...] = acc
            even = lax.rem(k, 2) == 0
            for p in (0, 2):
                @pl.when(even & (lay == 2 * frag + PIECES[p][0]))
                def _(p=p):
                    make_delta(p, lay)
                    make_delta(p + 1, lay)
            return 0

        lax.fori_loop(0, L, layer, 0)

    def sync(frag):
        for gi, (p, c, u0, nu) in enumerate(GROUPS):
            d0, d1, d2 = dims_of(c)
            k0 = coord[d0]
            rows = pl.ds(pl.multiple_of(core * 64 + k0 * 32, 32), 32)
            for cp in rs0_copies(gi):
                cp.wait_recv()
            for u in range(u0, u0 + nu):
                s1[p, u] = ((delta[p, u, rows, :].astype(F32) + raw[0, p, u].astype(F32))
                            + (raw[1, p, u].astype(F32) + raw[2, p, u].astype(F32)))
            stage_copy(RS1, gi).start()
        for gi, (p, c, u0, nu) in enumerate(GROUPS):
            d0, d1, d2 = dims_of(c)
            k1 = coord[d1]
            rows = pl.ds(pl.multiple_of(k1 * 16, 16), 16)
            stage_copy(RS1, gi).wait_recv()
            for u in range(u0, u0 + nu):
                s2[p, u] = s1[p, u, rows, :] + r1[p, u]
            stage_copy(RS2, gi).start()
        for gi, (p, c, u0, nu) in enumerate(GROUPS):
            d0, d1, d2 = dims_of(c)
            k0, k1, k2 = coord[d0], coord[d1], coord[d2]
            rows = pl.ds(pl.multiple_of(k2 * 8, 8), 8)
            out_rows = pl.ds(pl.multiple_of(core * 64 + k0 * 32 + k1 * 16 + k2 * 8, 8), 8)
            stage_copy(RS2, gi).wait_recv()
            for u in range(u0, u0 + nu):
                full[p, u, out_rows, :] = s2[p, u, rows, :] + r2[p, u]
            stage_copy(AG0, gi).start()
        for gi in range(12):
            stage_copy(AG0, gi).wait_recv()
            stage_copy(AG1, gi).start()
        for gi in range(12):
            stage_copy(AG1, gi).wait_recv()
            stage_copy(AG2, gi).start()
            stage_copy(DDA, gi).start()
        for gi in range(12):
            stage_copy(AG2, gi).wait_recv()
            stage_copy(DDB, gi).start()
        for p, (part, mat) in enumerate(PIECES):
            for gi in range(3 * p, 3 * p + 3):
                stage_copy(DDA, gi).wait_recv()
                stage_copy(DDB, gi).wait_recv()
            lay = 2 * frag + part
            wr, wbr, gr, mr = (w1, w1b, g1, m1) if mat == 1 else (w2, w2b, g2, m2)
            for u in range(8):
                rows, cols = unit_slice(mat, u)
                mean = full[p, u] * (1.0 / N_ALL)
                mom = OUTER_MOM * mr[lay, rows, cols] + mean
                glob = gr[lay, rows, cols] - OUTER_LR * (OUTER_MOM * mom + mean)
                mr[lay, rows, cols] = mom
                gr[lay, rows, cols] = glob
                merged = MERGE_MIX * wr[0, lay, rows, cols] + (1.0 - MERGE_MIX) * glob
                wr[0, lay, rows, cols] = merged
                wbr[lay, rows, cols] = merged.astype(BF16)
        for gi in range(12):
            for cp in rs0_copies(gi):
                cp.wait_send()
            for stage in range(7):
                stage_copy(stage, gi).wait_send()

    def step(k, _):
        forward(k)
        backward(k)

        @pl.when(lax.rem(k, 2) == 1)
        def _():
            sync(k // 2)
        return 0

    lax.fori_loop(0, H, step, 0)


def write_body(*refs):
    srcs, dsts, sem = refs[:6], refs[6:12], refs[12]
    cps = []
    for i in range(6):
        for lay in range(L):
            src = srcs[i].at[0, lay] if i < 2 else srcs[i].at[lay]
            dst = dsts[i].at[0, lay] if i < 2 else dsts[i].at[lay]
            cps.append(pltpu.make_async_copy(src, dst, sem.at[i, lay]))
    for cp in cps:
        cp.start()
    for cp in cps:
        cp.wait()


def solution(mesh):
    def device_fn(w1_loc, w2_loc, w1_glb, w2_glb, mom1, mom2, x_loc, y_loc):
        arrays = (w1_loc, w2_loc, w1_glb, w2_glb, mom1, mom2)
        shapes = [jax.ShapeDtypeStruct(a.shape, F32) for a in arrays]
        dma = pltpu.SemaphoreType.DMA
        work = pl.pallas_call(
            main_body,
            out_shape=shapes,
            in_specs=[ANY] * 8,
            out_specs=[VMEM] * 6,
            scratch_shapes=[
                pltpu.VMEM((H, B, D), BF16), pltpu.VMEM((H, B, D), BF16),
                pltpu.VMEM((L, D, FF), BF16), pltpu.VMEM((L, FF, D), BF16),
                pltpu.VMEM((L, B, D), BF16), pltpu.VMEM((L, B, FF), BF16), pltpu.VMEM((L, B, FF), F32),
                pltpu.VMEM((B, D), F32), pltpu.VMEM((B, D), F32),
                pltpu.VMEM((4, 8, 128, 256), BF16), pltpu.VMEM((3, 4, 8, 32, 256), BF16),
                pltpu.VMEM((4, 8, 32, 256), F32), pltpu.VMEM((4, 8, 16, 256), F32),
                pltpu.VMEM((4, 8, 16, 256), F32), pltpu.VMEM((4, 8, 8, 256), F32),
                pltpu.VMEM((4, 8, 128, 256), F32),
                dma((26,)), dma((12, 3)), dma((12, 3)), dma((7, 12)), dma((7, 12)),
            ],
            compiler_params=pltpu.CompilerParams(
                collective_id=0, has_side_effects=True, vmem_limit_bytes=28 * 2**20),
            name='diloco_round',
        )(*arrays, x_loc, y_loc)
        outs = pl.pallas_call(
            write_body,
            out_shape=shapes,
            in_specs=[VMEM] * 6,
            out_specs=[ANY] * 6,
            scratch_shapes=[dma((6, L))],
            compiler_params=pltpu.CompilerParams(vmem_limit_bytes=2 * 2**20),
            name='write_out',
        )(*work)
        return tuple(outs)

    local_spec = P(('shard', 'worker'))
    whole_spec = P()
    return jax.shard_map(device_fn, mesh=mesh, in_specs=(local_spec, local_spec, whole_spec, whole_spec, whole_spec, whole_spec, local_spec, local_spec), out_specs=(local_spec, local_spec, whole_spec, whole_spec, whole_spec, whole_spec), check_vma=False)
```

profile of v0, /device:TPU:0, one launch (start us, length us, event | category | flops | bytes accessed | tf_op | source)
XLA Modules:
  0.0 100.0 jit_solution(17545457774592915241)
XLA Ops:
  0.6 0.0 copy-start
  0.6 0.9 copy-done
  1.6 0.0 copy-start.1
  1.6 0.9 copy-done.1
  2.5 88.9 %diloco_round.1 = (f32[1,4,256,1024]{3,2,1,0:T(8,128)S(1)}, f32[1,4,1024,256]{3,2,1,0:T(8,128)S(1)}, f32[4,256,1024]{2,1,0:T(8,128)S(1)}, f32[4,1024,256]{2,1,0:...) custom-call(f32[1,4,256,1024]{3,2,1,0:T(8,128)} %w1_in.1, f32[1,4,1024,256]{3,2,1,0:T(8,128)} %w2_in.1, ...), custom_call_target="tpu_custom_call" | custom-call | tf_op jit(solution)/shard_map/diloco_round/pallas_call | solution.py:332
  91.5 8.6 %write_out.1 = (f32[1,4,256,1024]{3,2,1,0:T(8,128)}, f32[1,4,1024,256]{3,2,1,0:T(8,128)}, f32[4,256,1024]{2,1,0:T(8,128)}, f32[4,1024,256]{2,1,0:T(8,128)}, f32[...) custom-call(f32[1,4,256,1024]{3,2,1,0:T(8,128)S(1)} %get-tuple-element.12.refs_0_, ...), custom_call_target="tpu_custom_call" | custom-call | tf_op jit(solution)/shard_map/write_out/pallas_call | solution.py:352
Async XLA Ops:
  0.6 1.0 copy-start
  1.6 0.9 copy-start.1
where the time goes:
time: 100 us
  Pallas kernels  97.5 us (98%)
  local copies, waits for them, and re-layouts  1.89 us (2%)
    pallas_call x1, Pallas kernels, device_fn(): pl.pallas_call(main_body, out_shape=shapes, in_specs=[ANY] * 8, out_specs...  88.9 us
    pallas_call x1, Pallas kernels, device_fn(): pl.pallas_call(write_body, out_shape=shapes, in_specs=[VMEM] * 6, out_spe...  8.56 us

commit v1 on v0

--- a/solution.py
+++ b/solution.py
@@ -20,7 +20,7 @@
 F32 = jnp.float32
 BF16 = jnp.bfloat16
 MESH = pl.DeviceIdType.MESH
-ANY = pl.BlockSpec(memory_space=pl.ANY)
+HBM = pl.BlockSpec(memory_space=pltpu.HBM)
 VMEM = pl.BlockSpec(memory_space=pltpu.VMEM)
 
 PIECES = ((1, 2), (1, 1), (0, 2), (0, 1))
@@ -31,7 +31,7 @@
     for color in range(3):
         GROUPS.append((piece_idx, color, first_unit, COLOR_UNITS[piece_idx][color]))
         first_unit += COLOR_UNITS[piece_idx][color]
-RS1, RS2, AG0, AG1, AG2, DDA, DDB = range(7)
+RS1, X2, AG1, AG2, DDA, DDB = range(6)
 
 
 def dot(a, b, ca, cb):
@@ -40,11 +40,12 @@
 
 def gelu_pair(a):
     k0 = 0.7978845608028654
+    k1 = k0 * 0.044715
     a2 = a * a
-    t = jnp.tanh(k0 * (a + 0.044715 * (a2 * a)))
-    half = 0.5 * (1.0 + t)
-    u = a * half
-    du = half + (0.5 * a) * (1.0 - t * t) * (k0 * (1.0 + (3 * 0.044715) * a2))
+    t = jnp.tanh(a * (k0 + k1 * a2))
+    h = 0.5 + 0.5 * t
+    u = a * h
+    du = h + (u * (1.0 - h)) * (2.0 * k0 + (6.0 * k1) * a2)
     return u, du
 
 
@@ -81,44 +82,37 @@
         for same in (True, False):
             pl.semaphore_signal(bar, inc=1, device_id=chip_peer(dim, same), device_id_type=MESH)
 
-    def loads():
-        cps = [pltpu.make_async_copy(x_in.at[0], xb, ld_sem.at[24]),
-               pltpu.make_async_copy(y_in.at[0], yb, ld_sem.at[25])]
-        for lay in range(L):
-            cps.append(pltpu.make_async_copy(w1_in.at[0, lay], w1.at[0, lay], ld_sem.at[lay]))
-            cps.append(pltpu.make_async_copy(w2_in.at[0, lay], w2.at[0, lay], ld_sem.at[4 + lay]))
-        gcps = []
-        for lay in range(L):
-            gcps.append(pltpu.make_async_copy(g1_in.at[lay], g1.at[lay], ld_sem.at[8 + lay]))
-            gcps.append(pltpu.make_async_copy(g2_in.at[lay], g2.at[lay], ld_sem.at[12 + lay]))
-            gcps.append(pltpu.make_async_copy(m1_in.at[lay], m1.at[lay], ld_sem.at[16 + lay]))
-            gcps.append(pltpu.make_async_copy(m2_in.at[lay], m2.at[lay], ld_sem.at[20 + lay]))
-        return cps, gcps
-
-    cps, gcps = loads()
-    for cp in cps + gcps:
+    def w_load(lay):
+        return (pltpu.make_async_copy(w1_in.at[0, lay], w1.at[0, lay], ld_sem.at[lay]),
+                pltpu.make_async_copy(w2_in.at[0, lay], w2.at[0, lay], ld_sem.at[L + lay]))
+
+    def g_load(mat, lay):
+        if mat == 1:
+            return pltpu.make_async_copy(g1_in.at[lay], g1.at[lay], ld_sem.at[2 * L + lay])
+        return pltpu.make_async_copy(g2_in.at[lay], g2.at[lay], ld_sem.at[3 * L + lay])
+
+    def m_load(mat, lay):
+        if mat == 1:
+            return pltpu.make_async_copy(m1_in.at[lay], m1.at[lay], ld_sem.at[4 * L + lay])
+        return pltpu.make_async_copy(m2_in.at[lay], m2.at[lay], ld_sem.at[5 * L + lay])
+
+    x_load = pltpu.make_async_copy(x_in.at[0], xb, ld_sem.at[6 * L])
+    y_load = pltpu.make_async_copy(y_in.at[0], yb, ld_sem.at[6 * L + 1])
+    x_load.start()
+    for cp in w_load(0):
         cp.start()
-    cps[0].wait()
-    cps[1].wait()
+    y_load.start()
+    for lay in range(1, L):
+        for cp in w_load(lay):
+            cp.start()
     for lay in range(L):
-        cps[2 + 2 * lay].wait()
-        cps[3 + 2 * lay].wait()
-
-        def cast1(i, _, lay=lay):
-            rows = pl.ds(pl.multiple_of(i * 32, 32), 32)
-            w1b[lay, rows, :] = w1[0, lay, rows, :].astype(BF16)
-            return 0
-
-        def cast2(i, _, lay=lay):
-            rows = pl.ds(pl.multiple_of(i * 128, 128), 128)
-            w2b[lay, rows, :] = w2[0, lay, rows, :].astype(BF16)
-            return 0
-
-        lax.fori_loop(0, D // 32, cast1, 0)
-        lax.fori_loop(0, FF // 128, cast2, 0)
-    for cp in gcps:
-        cp.wait()
-    pl.semaphore_wait(bar, 7)
+        for mat in (1, 2):
+            g_load(mat, lay).start()
+    for lay in range(L):
+        for mat in (1, 2):
+            m_load(mat, lay).start()
+    x_load.wait()
+    y_load.wait()
 
     def dims_of(color_idx):
         return color_idx % 3, (color_idx + 1) % 3, (color_idx + 2) % 3
@@ -150,13 +144,11 @@
         us = pl.ds(u0, nu)
         if stage == RS1:
             src, dst, dev = s1.at[p, us, pl.ds(pl.multiple_of((1 - k1) * 16, 16), 16)], r1.at[p, us], chip_peer(d1)
-        elif stage == RS2:
-            src, dst, dev = s2.at[p, us, pl.ds(pl.multiple_of((1 - k2) * 8, 8), 8)], r2.at[p, us], chip_peer(d2)
+        elif stage == X2:
+            src, dst, dev = s2.at[p, us], r2.at[p, us], chip_peer(d2)
         else:
             base = core * 64
-            if stage == AG0:
-                off, n, dev = base + k0 * 32 + k1 * 16 + k2 * 8, 8, chip_peer(d2)
-            elif stage == AG1:
+            if stage == AG1:
                 off, n, dev = base + k0 * 32 + k1 * 16, 16, chip_peer(d1)
             elif stage == AG2:
                 off, n, dev = base + k0 * 32, 32, chip_peer(d0)
@@ -164,7 +156,7 @@
                 off, n, dev = base + k0 * 32, 32, partner
             else:
                 off, n, dev = base + (1 - k0) * 32, 32, partner
-            src = full.at[p, us, pl.ds(pl.multiple_of(off, 8), n)]
+            src = full.at[p, us, pl.ds(pl.multiple_of(off, 16), n)]
             dst = src
         return pltpu.make_async_remote_copy(
             src_ref=src, dst_ref=dst, send_sem=st_send.at[stage, gi], recv_sem=st_recv.at[stage, gi],
@@ -178,6 +170,7 @@
     def make_delta(p, lay):
         mat = PIECES[p][1]
         wr, gr = (w1, g1) if mat == 1 else (w2, g2)
+        g_load(mat, lay).wait()
         for u in range(8):
             rows, cols = unit_slice(mat, u)
             delta[p, u] = (gr[lay, rows, cols] - wr[0, lay, rows, cols]).astype(BF16)
@@ -189,6 +182,20 @@
         hid[...] = xb[k].astype(F32)
 
         def layer(lay, _):
+            @pl.when(k == 0)
+            def _():
+                for cp in w_load(lay):
+                    cp.wait()
+
+                def cast(i, _):
+                    rows = pl.ds(pl.multiple_of(i * 64, 64), 64)
+                    w1b[lay, rows, :] = w1[0, lay, rows, :].astype(BF16)
+                    rows = pl.ds(pl.multiple_of(i * 256, 256), 256)
+                    w2b[lay, rows, :] = w2[0, lay, rows, :].astype(BF16)
+                    return 0
+
+                lax.fori_loop(0, 4, cast, 0)
+
             h_bf = hid[...].astype(BF16)
             hb[lay] = h_bf
             acc = hid[...]
@@ -256,18 +263,13 @@
             stage_copy(RS1, gi).wait_recv()
             for u in range(u0, u0 + nu):
                 s2[p, u] = s1[p, u, rows, :] + r1[p, u]
-            stage_copy(RS2, gi).start()
+            stage_copy(X2, gi).start()
         for gi, (p, c, u0, nu) in enumerate(GROUPS):
             d0, d1, d2 = dims_of(c)
-            k0, k1, k2 = coord[d0], coord[d1], coord[d2]
-            rows = pl.ds(pl.multiple_of(k2 * 8, 8), 8)
-            out_rows = pl.ds(pl.multiple_of(core * 64 + k0 * 32 + k1 * 16 + k2 * 8, 8), 8)
-            stage_copy(RS2, gi).wait_recv()
+            rows = pl.ds(pl.multiple_of(core * 64 + coord[d0] * 32 + coord[d1] * 16, 16), 16)
+            stage_copy(X2, gi).wait_recv()
             for u in range(u0, u0 + nu):
-                full[p, u, out_rows, :] = s2[p, u, rows, :] + r2[p, u]
-            stage_copy(AG0, gi).start()
-        for gi in range(12):
-            stage_copy(AG0, gi).wait_recv()
+                full[p, u, rows, :] = s2[p, u] + r2[p, u]
             stage_copy(AG1, gi).start()
         for gi in range(12):
             stage_copy(AG1, gi).wait_recv()
@@ -282,6 +284,7 @@
                 stage_copy(DDB, gi).wait_recv()
             lay = 2 * frag + part
             wr, wbr, gr, mr = (w1, w1b, g1, m1) if mat == 1 else (w2, w2b, g2, m2)
+            m_load(mat, lay).wait()
             for u in range(8):
                 rows, cols = unit_slice(mat, u)
                 mean = full[p, u] * (1.0 / N_ALL)
@@ -295,11 +298,16 @@
         for gi in range(12):
             for cp in rs0_copies(gi):
                 cp.wait_send()
-            for stage in range(7):
+            for stage in range(6):
                 stage_copy(stage, gi).wait_send()
 
     def step(k, _):
         forward(k)
+
+        @pl.when(k == 0)
+        def _():
+            pl.semaphore_wait(bar, 7)
+
         backward(k)
 
         @pl.when(lax.rem(k, 2) == 1)
@@ -332,7 +340,7 @@
         work = pl.pallas_call(
             main_body,
             out_shape=shapes,
-            in_specs=[ANY] * 8,
+            in_specs=[HBM] * 8,
             out_specs=[VMEM] * 6,
             scratch_shapes=[
                 pltpu.VMEM((H, B, D), BF16), pltpu.VMEM((H, B, D), BF16),
@@ -341,19 +349,19 @@
                 pltpu.VMEM((B, D), F32), pltpu.VMEM((B, D), F32),
                 pltpu.VMEM((4, 8, 128, 256), BF16), pltpu.VMEM((3, 4, 8, 32, 256), BF16),
                 pltpu.VMEM((4, 8, 32, 256), F32), pltpu.VMEM((4, 8, 16, 256), F32),
-                pltpu.VMEM((4, 8, 16, 256), F32), pltpu.VMEM((4, 8, 8, 256), F32),
+                pltpu.VMEM((4, 8, 16, 256), F32), pltpu.VMEM((4, 8, 16, 256), F32),
                 pltpu.VMEM((4, 8, 128, 256), F32),
-                dma((26,)), dma((12, 3)), dma((12, 3)), dma((7, 12)), dma((7, 12)),
+                dma((26,)), dma((12, 3)), dma((12, 3)), dma((6, 12)), dma((6, 12)),
             ],
             compiler_params=pltpu.CompilerParams(
                 collective_id=0, has_side_effects=True, vmem_limit_bytes=28 * 2**20),
             name='diloco_round',
-        )(*arrays, x_loc, y_loc)
+        )(*[pltpu.with_memory_space_constraint(a, pltpu.HBM) for a in (*arrays, x_loc, y_loc)])
         outs = pl.pallas_call(
             write_body,
             out_shape=shapes,
             in_specs=[VMEM] * 6,
-            out_specs=[ANY] * 6,
+            out_specs=[HBM] * 6,
             scratch_shapes=[dma((6, L))],
             compiler_params=pltpu.CompilerParams(vmem_limit_bytes=2 * 2**20),
             name='write_out',

time: 100 us -> 88.1 us (0.88)
  Pallas kernels: 97.5 us -> 87.3 us
  local copies, waits for them, and re-layouts: 1.89 us -> 0 us
    pallas_call x1, Pallas kernels: 88.9 us -> 78.7 us  [device_fn(): pl.pallas_call(main_body, out_shape=shapes, in_specs=[HBM] * 8, out_specs...]
    unnamed x4 -> x0, local copies, waits for them, and re-layouts: 1.89 us -> none
where the time goes in v1:
time: 88.1 us; the launch traced here: 87.9 us
  Pallas kernels  87.3 us (99%)
    pallas_call x1, Pallas kernels, device_fn(): pl.pallas_call(main_body, out_shape=shapes, in_specs=[HBM] * 8, out_specs...  78.7 us
    pallas_call x1, Pallas kernels, device_fn(): pl.pallas_call(write_body, out_shape=shapes, in_specs=[VMEM] * 6, out_spe...  8.56 us

profile of v1, /device:TPU:0, one launch (start us, length us, event | category | flops | bytes accessed | tf_op | source)
XLA Modules:
  0.0 87.9 jit_solution(6050789727937005399)
XLA Ops:
  0.6 78.7 %diloco_round.1 = (f32[1,4,256,1024]{3,2,1,0:T(8,128)S(1)}, f32[1,4,1024,256]{3,2,1,0:T(8,128)S(1)}, f32[4,256,1024]{2,1,0:T(8,128)S(1)}, f32[4,1024,256]{2,1,0:...) custom-call(f32[1,4,256,1024]{3,2,1,0:T(8,128)} %w1_in.1, f32[1,4,1024,256]{3,2,1,0:T(8,128)} %w2_in.1, ...), custom_call_target="tpu_custom_call" | custom-call | tf_op jit(solution)/shard_map/diloco_round/pallas_call | solution.py:340
  79.4 8.6 %write_out.1 = (f32[1,4,256,1024]{3,2,1,0:T(8,128)}, f32[1,4,1024,256]{3,2,1,0:T(8,128)}, f32[4,256,1024]{2,1,0:T(8,128)}, f32[4,1024,256]{2,1,0:T(8,128)}, f32[...) custom-call(f32[1,4,256,1024]{3,2,1,0:T(8,128)S(1)} %get-tuple-element.12.refs_0_, ...), custom_call_target="tpu_custom_call" | custom-call | tf_op jit(solution)/shard_map/write_out/pallas_call | solution.py:360

commit v2 on v1

--- a/solution.py
+++ b/solution.py
@@ -31,6 +31,7 @@
     for color in range(3):
         GROUPS.append((piece_idx, color, first_unit, COLOR_UNITS[piece_idx][color]))
         first_unit += COLOR_UNITS[piece_idx][color]
+GATHER_ORDER = (0, 2, 3, 1)
 RS1, X2, AG1, AG2, DDA, DDB = range(6)
 
 
@@ -51,7 +52,7 @@
 
 def main_body(w1_in, w2_in, g1_in, g2_in, m1_in, m2_in, x_in, y_in,
               w1, w2, g1, g2, m1, m2,
-              xb, yb, w1b, w2b, hb, ub, du, hid, dhid,
+              xb, yb, w1b, w2b, hb, ub, du, hid, dhid, eb, cb,
               delta, raw, s1, r1, s2, r2, full,
               ld_sem, s0_send, s0_recv, st_send, st_recv):
     zc = lax.axis_index('shard')
@@ -178,24 +179,27 @@
             for cp in rs0_copies(gi):
                 cp.start()
 
-    def forward(k):
+    def cast_layer(lay):
+        for cp in w_load(lay):
+            cp.wait()
+
+        def cast(i, _):
+            rows = pl.ds(pl.multiple_of(i * 64, 64), 64)
+            w1b[lay, rows, :] = w1[0, lay, rows, :].astype(BF16)
+            rows = pl.ds(pl.multiple_of(i * 256, 256), 256)
+            w2b[lay, rows, :] = w2[0, lay, rows, :].astype(BF16)
+            return 0
+
+        lax.fori_loop(0, 4, cast, 0)
+
+    def forward(k, before_layer_1=None):
         hid[...] = xb[k].astype(F32)
 
         def layer(lay, _):
-            @pl.when(k == 0)
-            def _():
-                for cp in w_load(lay):
-                    cp.wait()
-
-                def cast(i, _):
-                    rows = pl.ds(pl.multiple_of(i * 64, 64), 64)
-                    w1b[lay, rows, :] = w1[0, lay, rows, :].astype(BF16)
-                    rows = pl.ds(pl.multiple_of(i * 256, 256), 256)
-                    w2b[lay, rows, :] = w2[0, lay, rows, :].astype(BF16)
-                    return 0
-
-                lax.fori_loop(0, 4, cast, 0)
-
+            if k == 0:
+                cast_layer(lay)
+            if before_layer_1 is not None:
+                pl.when(lay == 1)(before_layer_1)
             h_bf = hid[...].astype(BF16)
             hb[lay] = h_bf
             acc = hid[...]
@@ -212,110 +216,193 @@
 
         lax.fori_loop(0, L, layer, 0)
 
-    def backward(k):
-        frag = k // 2
+    def loss_grad(k):
         dhid[...] = (2.0 / (B * D)) * (hid[...] - yb[k].astype(F32))
 
-        def layer(li, _):
-            lay = (L - 1) - li
-            e = dhid[...].astype(BF16)
-            h_bf = hb[lay]
-            acc = dhid[...]
-            for j in range(NB):
-                cols = slice(j * D, (j + 1) * D)
-                d_u = dot(e, w2b[lay, cols, :], 1, 1)
-                c = (du[lay, :, cols] * d_u).astype(BF16)
-                g_w2 = dot(ub[lay, :, cols], e, 0, 0)
-                new2 = w2[0, lay, cols, :] - INNER_LR * g_w2
-                w2[0, lay, cols, :] = new2
-                w2b[lay, cols, :] = new2.astype(BF16)
-                acc = acc + dot(c, w1b[lay, :, cols], 1, 1)
-                g_w1 = dot(h_bf, c, 0, 0)
-                new1 = w1[0, lay, :, cols] - INNER_LR * g_w1
-                w1[0, lay, :, cols] = new1
-                w1b[lay, :, cols] = new1.astype(BF16)
-            dhid[...] = acc
-            even = lax.rem(k, 2) == 0
-            for p in (0, 2):
-                @pl.when(even & (lay == 2 * frag + PIECES[p][0]))
-                def _(p=p):
-                    make_delta(p, lay)
-                    make_delta(p + 1, lay)
-            return 0
-
-        lax.fori_loop(0, L, layer, 0)
-
-    def sync(frag):
-        for gi, (p, c, u0, nu) in enumerate(GROUPS):
-            d0, d1, d2 = dims_of(c)
-            k0 = coord[d0]
-            rows = pl.ds(pl.multiple_of(core * 64 + k0 * 32, 32), 32)
+    def update2(lay, cols, u_j, e):
+        new2 = w2[0, lay, cols, :] - INNER_LR * dot(u_j, e, 0, 0)
+        w2[0, lay, cols, :] = new2
+        w2b[lay, cols, :] = new2.astype(BF16)
+
+    def update1(lay, cols, h_bf, c):
+        new1 = w1[0, lay, :, cols] - INNER_LR * dot(h_bf, c, 0, 0)
+        w1[0, lay, :, cols] = new1
+        w1b[lay, :, cols] = new1.astype(BF16)
+
+    def back_full(lay):
+        e = dhid[...].astype(BF16)
+        h_bf = hb[lay]
+        acc = dhid[...]
+        for j in range(NB):
+            cols = slice(j * D, (j + 1) * D)
+            d_u = dot(e, w2b[lay, cols, :], 1, 1)
+            c = (du[lay, :, cols] * d_u).astype(BF16)
+            update2(lay, cols, ub[lay, :, cols], e)
+            acc = acc + dot(c, w1b[lay, :, cols], 1, 1)
+            update1(lay, cols, h_bf, c)
+        dhid[...] = acc
+
+    def back_chain(lay):
+        e = dhid[...].astype(BF16)
+        eb[lay - 2] = e
+        acc = dhid[...]
+        for j in range(NB):
+            cols = slice(j * D, (j + 1) * D)
+            d_u = dot(e, w2b[lay, cols, :], 1, 1)
+            c = (du[lay, :, cols] * d_u).astype(BF16)
+            cb[lay - 2, :, cols] = c
+            acc = acc + dot(c, w1b[lay, :, cols], 1, 1)
+        dhid[...] = acc
+
+    def back_weights(lay):
+        e = eb[lay - 2]
+        h_bf = hb[lay]
+        for j in range(NB):
+            cols = slice(j * D, (j + 1) * D)
+            update2(lay, cols, ub[lay, :, cols], e)
+            update1(lay, cols, h_bf, cb[lay - 2, :, cols])
+
+    def reduce_stage1(p):
+        for gi in range(3 * p, 3 * p + 3):
+            _, c, u0, nu = GROUPS[gi]
+            rows = pl.ds(pl.multiple_of(core * 64 + coord[dims_of(c)[0]] * 32, 32), 32)
             for cp in rs0_copies(gi):
                 cp.wait_recv()
             for u in range(u0, u0 + nu):
                 s1[p, u] = ((delta[p, u, rows, :].astype(F32) + raw[0, p, u].astype(F32))
                             + (raw[1, p, u].astype(F32) + raw[2, p, u].astype(F32)))
             stage_copy(RS1, gi).start()
-        for gi, (p, c, u0, nu) in enumerate(GROUPS):
-            d0, d1, d2 = dims_of(c)
-            k1 = coord[d1]
-            rows = pl.ds(pl.multiple_of(k1 * 16, 16), 16)
+
+    def reduce_stage2(p):
+        for gi in range(3 * p, 3 * p + 3):
+            _, c, u0, nu = GROUPS[gi]
+            rows = pl.ds(pl.multiple_of(coord[dims_of(c)[1]] * 16, 16), 16)
             stage_copy(RS1, gi).wait_recv()
             for u in range(u0, u0 + nu):
                 s2[p, u] = s1[p, u, rows, :] + r1[p, u]
             stage_copy(X2, gi).start()
-        for gi, (p, c, u0, nu) in enumerate(GROUPS):
+
+    def reduce_stage3(p):
+        for gi in range(3 * p, 3 * p + 3):
+            _, c, u0, nu = GROUPS[gi]
             d0, d1, d2 = dims_of(c)
             rows = pl.ds(pl.multiple_of(core * 64 + coord[d0] * 32 + coord[d1] * 16, 16), 16)
             stage_copy(X2, gi).wait_recv()
             for u in range(u0, u0 + nu):
                 full[p, u, rows, :] = s2[p, u] + r2[p, u]
             stage_copy(AG1, gi).start()
-        for gi in range(12):
+
+    def gather_stage2(p):
+        for gi in range(3 * p, 3 * p + 3):
             stage_copy(AG1, gi).wait_recv()
             stage_copy(AG2, gi).start()
             stage_copy(DDA, gi).start()
-        for gi in range(12):
+
+    def gather_stage3(p):
+        for gi in range(3 * p, 3 * p + 3):
             stage_copy(AG2, gi).wait_recv()
             stage_copy(DDB, gi).start()
-        for p, (part, mat) in enumerate(PIECES):
-            for gi in range(3 * p, 3 * p + 3):
-                stage_copy(DDA, gi).wait_recv()
-                stage_copy(DDB, gi).wait_recv()
-            lay = 2 * frag + part
-            wr, wbr, gr, mr = (w1, w1b, g1, m1) if mat == 1 else (w2, w2b, g2, m2)
-            m_load(mat, lay).wait()
-            for u in range(8):
-                rows, cols = unit_slice(mat, u)
-                mean = full[p, u] * (1.0 / N_ALL)
-                mom = OUTER_MOM * mr[lay, rows, cols] + mean
-                glob = gr[lay, rows, cols] - OUTER_LR * (OUTER_MOM * mom + mean)
-                mr[lay, rows, cols] = mom
-                gr[lay, rows, cols] = glob
-                merged = MERGE_MIX * wr[0, lay, rows, cols] + (1.0 - MERGE_MIX) * glob
-                wr[0, lay, rows, cols] = merged
-                wbr[lay, rows, cols] = merged.astype(BF16)
+
+    def outer_update(frag, p):
+        part, mat = PIECES[p]
+        lay = 2 * frag + part
+        wr, wbr, gr, mr = (w1, w1b, g1, m1) if mat == 1 else (w2, w2b, g2, m2)
+        m_load(mat, lay).wait()
+        for gi in range(3 * p, 3 * p + 3):
+            stage_copy(DDA, gi).wait_recv()
+            stage_copy(DDB, gi).wait_recv()
+        for u in range(8):
+            rows, cols = unit_slice(mat, u)
+            mean = full[p, u] * (1.0 / N_ALL)
+            mom = OUTER_MOM * mr[lay, rows, cols] + mean
+            glob = gr[lay, rows, cols] - OUTER_LR * (OUTER_MOM * mom + mean)
+            mr[lay, rows, cols] = mom
+            gr[lay, rows, cols] = glob
+            merged = MERGE_MIX * wr[0, lay, rows, cols] + (1.0 - MERGE_MIX) * glob
+            wr[0, lay, rows, cols] = merged
+            wbr[lay, rows, cols] = merged.astype(BF16)
+
+    last_piece = GATHER_ORDER[-1]
+
+    def finish(frag):
+        outer_update(frag, last_piece)
         for gi in range(12):
             for cp in rs0_copies(gi):
                 cp.wait_send()
             for stage in range(6):
                 stage_copy(stage, gi).wait_send()
 
-    def step(k, _):
-        forward(k)
-
-        @pl.when(k == 0)
+    def sync(frag):
+        reduce_stage1(3)
+        for p in range(4):
+            reduce_stage2(p)
+        for p in range(4):
+            reduce_stage3(p)
+        for p in GATHER_ORDER:
+            gather_stage2(p)
+        prev = None
+        for p in GATHER_ORDER:
+            gather_stage3(p)
+            if prev is not None:
+                outer_update(frag, prev)
+            prev = p
+
+    def layers(lo, body):
+        def run(i, _):
+            body(i, lo - i)
+            return 0
+        return run
+
+    def send_layer(lay, part):
+        for p in (0, 2):
+            @pl.when(part == PIECES[p][0])
+            def _(p=p):
+                make_delta(p, lay)
+                make_delta(p + 1, lay)
+
+    forward(0)
+    pl.semaphore_wait(bar, 7)
+    loss_grad(0)
+    lax.fori_loop(0, 2, layers(3, lambda i, lay: back_chain(lay)), 0)
+
+    def back_send_0(i, lay):
+        back_full(lay)
+        send_layer(lay, lay)
+
+    lax.fori_loop(0, 2, layers(1, back_send_0), 0)
+    lax.fori_loop(0, 2, layers(3, lambda i, lay: back_weights(lay)), 0)
+
+    def back_hook(i, lay):
+        back_full(lay)
+
+        @pl.when(i == 0)
         def _():
-            pl.semaphore_wait(bar, 7)
-
-        backward(k)
-
-        @pl.when(lax.rem(k, 2) == 1)
+            reduce_stage1(0)
+            reduce_stage1(1)
+
+        @pl.when(i == 2)
         def _():
-            sync(k // 2)
-        return 0
-
-    lax.fori_loop(0, H, step, 0)
+            reduce_stage1(2)
+
+    forward(1)
+    loss_grad(1)
+    lax.fori_loop(0, L, layers(3, back_hook), 0)
+    sync(0)
+
+    forward(2, lambda: finish(0))
+    loss_grad(2)
+
+    def back_send_1(i, lay):
+        back_full(lay)
+        pl.when(i < 2)(lambda: send_layer(lay, lay - 2))
+
+    lax.fori_loop(0, L, layers(3, back_send_1), 0)
+
+    forward(3)
+    loss_grad(3)
+    lax.fori_loop(0, L, layers(3, back_hook), 0)
+    sync(1)
+    finish(1)
 
 
 def write_body(*refs):
@@ -347,6 +434,7 @@
                 pltpu.VMEM((L, D, FF), BF16), pltpu.VMEM((L, FF, D), BF16),
                 pltpu.VMEM((L, B, D), BF16), pltpu.VMEM((L, B, FF), BF16), pltpu.VMEM((L, B, FF), F32),
                 pltpu.VMEM((B, D), F32), pltpu.VMEM((B, D), F32),
+                pltpu.VMEM((2, B, D), BF16), pltpu.VMEM((2, B, FF), BF16),
                 pltpu.VMEM((4, 8, 128, 256), BF16), pltpu.VMEM((3, 4, 8, 32, 256), BF16),
                 pltpu.VMEM((4, 8, 32, 256), F32), pltpu.VMEM((4, 8, 16, 256), F32),
                 pltpu.VMEM((4, 8, 16, 256), F32), pltpu.VMEM((4, 8, 16, 256), F32),

time: 88.1 us -> 84 us (0.953)
  Pallas kernels: 87.3 us -> 82.9 us
    pallas_call x1, Pallas kernels: 78.7 us -> 74.4 us  [device_fn(): pl.pallas_call(main_body, out_shape=shapes, in_specs=[HBM] * 8, out_specs...]
where the time goes in v2:
time: 84 us; the launch traced here: 83.7 us
  Pallas kernels  82.9 us (99%)
    pallas_call x1, Pallas kernels, device_fn(): pl.pallas_call(main_body, out_shape=shapes, in_specs=[HBM] * 8, out_specs...  74.4 us
    pallas_call x1, Pallas kernels, device_fn(): pl.pallas_call(write_body, out_shape=shapes, in_specs=[VMEM] * 6, out_spe...  8.56 us

profile of v2, /device:TPU:0, one launch (start us, length us, event | category | flops | bytes accessed | tf_op | source)
XLA Modules:
  0.0 83.7 jit_solution(14138511136734749693)
XLA Ops:
  0.6 74.4 %diloco_round.1 = (f32[1,4,256,1024]{3,2,1,0:T(8,128)S(1)}, f32[1,4,1024,256]{3,2,1,0:T(8,128)S(1)}, f32[4,256,1024]{2,1,0:T(8,128)S(1)}, f32[4,1024,256]{2,1,0:...) custom-call(f32[1,4,256,1024]{3,2,1,0:T(8,128)} %w1_in.1, f32[1,4,1024,256]{3,2,1,0:T(8,128)} %w2_in.1, ...), custom_call_target="tpu_custom_call" | custom-call | tf_op jit(solution)/shard_map/diloco_round/pallas_call | solution.py:427
  75.0 8.6 %write_out.1 = (f32[1,4,256,1024]{3,2,1,0:T(8,128)}, f32[1,4,1024,256]{3,2,1,0:T(8,128)}, f32[4,256,1024]{2,1,0:T(8,128)}, f32[4,1024,256]{2,1,0:T(8,128)}, f32[...) custom-call(f32[1,4,256,1024]{3,2,1,0:T(8,128)S(1)} %get-tuple-element.12.refs_0_, ...), custom_call_target="tpu_custom_call" | custom-call | tf_op jit(solution)/shard_map/write_out/pallas_call | solution.py:448

commit v3 on v2

--- a/solution.py
+++ b/solution.py
@@ -32,6 +32,7 @@
         GROUPS.append((piece_idx, color, first_unit, COLOR_UNITS[piece_idx][color]))
         first_unit += COLOR_UNITS[piece_idx][color]
 GATHER_ORDER = (0, 2, 3, 1)
+LAST = GATHER_ORDER[-1]
 RS1, X2, AG1, AG2, DDA, DDB = range(6)
 
 
@@ -54,7 +55,7 @@
               w1, w2, g1, g2, m1, m2,
               xb, yb, w1b, w2b, hb, ub, du, hid, dhid, eb, cb,
               delta, raw, s1, r1, s2, r2, full,
-              ld_sem, s0_send, s0_recv, st_send, st_recv):
+              ld_sem, s0_send, s0_recv, st_send, st_recv, un_send, un_recv):
     zc = lax.axis_index('shard')
     wk = lax.axis_index('worker')
     core = lax.rem(wk, 2)
@@ -113,7 +114,6 @@
         for mat in (1, 2):
             m_load(mat, lay).start()
     x_load.wait()
-    y_load.wait()
 
     def dims_of(color_idx):
         return color_idx % 3, (color_idx + 1) % 3, (color_idx + 2) % 3
@@ -168,36 +168,32 @@
             return pl.ds(u * 128, 128), pl.ds(0, 256)
         return pl.ds((u % 2) * 128, 128), pl.ds((u // 2) * 256, 256)
 
-    def make_delta(p, lay):
-        mat = PIECES[p][1]
-        wr, gr = (w1, g1) if mat == 1 else (w2, g2)
-        g_load(mat, lay).wait()
-        for u in range(8):
-            rows, cols = unit_slice(mat, u)
-            delta[p, u] = (gr[lay, rows, cols] - wr[0, lay, rows, cols]).astype(BF16)
-        for gi in range(3 * p, 3 * p + 3):
-            for cp in rs0_copies(gi):
-                cp.start()
-
-    def cast_layer(lay):
-        for cp in w_load(lay):
-            cp.wait()
-
-        def cast(i, _):
-            rows = pl.ds(pl.multiple_of(i * 64, 64), 64)
-            w1b[lay, rows, :] = w1[0, lay, rows, :].astype(BF16)
-            rows = pl.ds(pl.multiple_of(i * 256, 256), 256)
-            w2b[lay, rows, :] = w2[0, lay, rows, :].astype(BF16)
-            return 0
-
-        lax.fori_loop(0, 4, cast, 0)
+    def layer_0(lay, _):
+        load1, load2 = w_load(lay)
+        h_bf = hid[...].astype(BF16)
+        hb[lay] = h_bf
+        load1.wait()
+        for j in range(NB):
+            cols = slice(j * D, (j + 1) * D)
+            w_bf = w1[0, lay, :, cols].astype(BF16)
+            w1b[lay, :, cols] = w_bf
+            u, dg = gelu_pair(dot(h_bf, w_bf, 1, 0))
+            ub[lay, :, cols] = u.astype(BF16)
+            du[lay, :, cols] = dg
+        load2.wait()
+        acc = hid[...]
+        for j in range(NB):
+            cols = slice(j * D, (j + 1) * D)
+            w_bf = w2[0, lay, cols, :].astype(BF16)
+            w2b[lay, cols, :] = w_bf
+            acc = acc + dot(ub[lay, :, cols], w_bf, 1, 0)
+        hid[...] = acc
+        return 0
 
     def forward(k, before_layer_1=None):
         hid[...] = xb[k].astype(F32)
 
         def layer(lay, _):
-            if k == 0:
-                cast_layer(lay)
             if before_layer_1 is not None:
                 pl.when(lay == 1)(before_layer_1)
             h_bf = hid[...].astype(BF16)
@@ -214,7 +210,7 @@
             hid[...] = acc
             return 0
 
-        lax.fori_loop(0, L, layer, 0)
+        lax.fori_loop(0, L, layer_0 if k == 0 else layer, 0)
 
     def loss_grad(k):
         dhid[...] = (2.0 / (B * D)) * (hid[...] - yb[k].astype(F32))
@@ -228,6 +224,44 @@
         new1 = w1[0, lay, :, cols] - INNER_LR * dot(h_bf, c, 0, 0)
         w1[0, lay, :, cols] = new1
         w1b[lay, :, cols] = new1.astype(BF16)
+
+    def send_piece(i, which):
+        for p in (which, 2 + which):
+            @pl.when(i == p // 2)
+            def _(p=p):
+                for gi in range(3 * p, 3 * p + 3):
+                    for cp in rs0_copies(gi):
+                        cp.start()
+
+    def back_send(i, lay):
+        p = 2 * i
+        e = dhid[...].astype(BF16)
+        h_bf = hb[lay]
+        g_load(2, lay).wait()
+        for j in range(NB):
+            cols = slice(j * D, (j + 1) * D)
+            new2 = w2[0, lay, cols, :] - INNER_LR * dot(ub[lay, :, cols], e, 0, 0)
+            w2[0, lay, cols, :] = new2
+            dl = (g2[lay, cols, :] - new2).astype(BF16)
+            delta[p, 2 * j] = dl[:128]
+            delta[p, 2 * j + 1] = dl[128:]
+        send_piece(i, 0)
+        g_load(1, lay).wait()
+        acc = dhid[...]
+        for j in range(NB):
+            cols = slice(j * D, (j + 1) * D)
+            d_u = dot(e, w2b[lay, cols, :], 1, 1)
+            c = (du[lay, :, cols] * d_u).astype(BF16)
+            acc = acc + dot(c, w1b[lay, :, cols], 1, 1)
+            new1 = w1[0, lay, :, cols] - INNER_LR * dot(h_bf, c, 0, 0)
+            w1[0, lay, :, cols] = new1
+            w1b[lay, :, cols] = new1.astype(BF16)
+            dl = (g1[lay, :, cols] - new1).astype(BF16)
+            delta[p + 1, 2 * j] = dl[:128]
+            delta[p + 1, 2 * j + 1] = dl[128:]
+        dhid[...] = acc
+        send_piece(i, 1)
+        w2b[lay] = w2[0, lay].astype(BF16)
 
     def back_full(lay):
         e = dhid[...].astype(BF16)
@@ -292,10 +326,25 @@
                 full[p, u, rows, :] = s2[p, u] + r2[p, u]
             stage_copy(AG1, gi).start()
 
+    def unit_copy(second, u):
+        p = LAST
+        d0 = dims_of([c for q, c, u0, nu in GROUPS if q == p and u0 <= u < u0 + nu][0])[0]
+        k0 = coord[d0]
+        off = core * 64 + ((1 - k0) if second else k0) * 32
+        ref = full.at[p, u, pl.ds(pl.multiple_of(off, 16), 32)]
+        return pltpu.make_async_remote_copy(
+            src_ref=ref, dst_ref=ref, send_sem=un_send.at[second, u], recv_sem=un_recv.at[second, u],
+            device_id=partner if second else chip_peer(d0), device_id_type=MESH)
+
     def gather_stage2(p):
         for gi in range(3 * p, 3 * p + 3):
             stage_copy(AG1, gi).wait_recv()
-            stage_copy(AG2, gi).start()
+            if p != LAST:
+                stage_copy(AG2, gi).start()
+            else:
+                _, _, u0, nu = GROUPS[gi]
+                for u in range(u0, u0 + nu):
+                    unit_copy(0, u).start()
             stage_copy(DDA, gi).start()
 
     def gather_stage3(p):
@@ -303,34 +352,55 @@
             stage_copy(AG2, gi).wait_recv()
             stage_copy(DDB, gi).start()
 
-    def outer_update(frag, p):
+    def outer_unit(frag, p, u):
         part, mat = PIECES[p]
         lay = 2 * frag + part
         wr, wbr, gr, mr = (w1, w1b, g1, m1) if mat == 1 else (w2, w2b, g2, m2)
-        m_load(mat, lay).wait()
+        rows, cols = unit_slice(mat, u)
+        mean = full[p, u] * (1.0 / N_ALL)
+        mom = OUTER_MOM * mr[lay, rows, cols] + mean
+        glob = gr[lay, rows, cols] - OUTER_LR * (OUTER_MOM * mom + mean)
+        mr[lay, rows, cols] = mom
+        gr[lay, rows, cols] = glob
+        merged = MERGE_MIX * wr[0, lay, rows, cols] + (1.0 - MERGE_MIX) * glob
+        wr[0, lay, rows, cols] = merged
+        if frag == 0:
+            wbr[lay, rows, cols] = merged.astype(BF16)
+
+    def load_momentum(frag, p):
+        part, mat = PIECES[p]
+        m_load(mat, 2 * frag + part).wait()
+
+    def outer_update(frag, p):
+        load_momentum(frag, p)
         for gi in range(3 * p, 3 * p + 3):
             stage_copy(DDA, gi).wait_recv()
             stage_copy(DDB, gi).wait_recv()
         for u in range(8):
-            rows, cols = unit_slice(mat, u)
-            mean = full[p, u] * (1.0 / N_ALL)
-            mom = OUTER_MOM * mr[lay, rows, cols] + mean
-            glob = gr[lay, rows, cols] - OUTER_LR * (OUTER_MOM * mom + mean)
-            mr[lay, rows, cols] = mom
-            gr[lay, rows, cols] = glob
-            merged = MERGE_MIX * wr[0, lay, rows, cols] + (1.0 - MERGE_MIX) * glob
-            wr[0, lay, rows, cols] = merged
-            wbr[lay, rows, cols] = merged.astype(BF16)
-
-    last_piece = GATHER_ORDER[-1]
+            outer_unit(frag, p, u)
 
     def finish(frag):
-        outer_update(frag, last_piece)
+        load_momentum(frag, LAST)
+        first = [(u0, u0 + nu) for q, c, u0, nu in GROUPS if q == LAST]
+        order = [u0 + i for i in range(3) for u0, end in first if u0 + i < end]
+        for gi in range(3 * LAST, 3 * LAST + 3):
+            stage_copy(DDA, gi).wait_recv()
+        for idx in range(8 + 3):
+            if idx < 8:
+                unit_copy(0, order[idx]).wait_recv()
+                unit_copy(1, order[idx]).start()
+            if idx >= 3:
+                unit_copy(1, order[idx - 3]).wait_recv()
+                outer_unit(frag, LAST, order[idx - 3])
         for gi in range(12):
             for cp in rs0_copies(gi):
                 cp.wait_send()
             for stage in range(6):
-                stage_copy(stage, gi).wait_send()
+                if GROUPS[gi][0] != LAST or stage not in (AG2, DDB):
+                    stage_copy(stage, gi).wait_send()
+        for u in range(8):
+            unit_copy(0, u).wait_send()
+            unit_copy(1, u).wait_send()
 
     def sync(frag):
         reduce_stage1(3)
@@ -341,11 +411,12 @@
         for p in GATHER_ORDER:
             gather_stage2(p)
         prev = None
-        for p in GATHER_ORDER:
+        for p in GATHER_ORDER[:-1]:
             gather_stage3(p)
             if prev is not None:
                 outer_update(frag, prev)
             prev = p
+        outer_update(frag, prev)
 
     def layers(lo, body):
         def run(i, _):
@@ -353,23 +424,13 @@
             return 0
         return run
 
-    def send_layer(lay, part):
-        for p in (0, 2):
-            @pl.when(part == PIECES[p][0])
-            def _(p=p):
-                make_delta(p, lay)
-                make_delta(p + 1, lay)
-
     forward(0)
+    y_load.wait()
     pl.semaphore_wait(bar, 7)
     loss_grad(0)
     lax.fori_loop(0, 2, layers(3, lambda i, lay: back_chain(lay)), 0)
 
-    def back_send_0(i, lay):
-        back_full(lay)
-        send_layer(lay, lay)
-
-    lax.fori_loop(0, 2, layers(1, back_send_0), 0)
+    lax.fori_loop(0, 2, layers(1, back_send), 0)
     lax.fori_loop(0, 2, layers(3, lambda i, lay: back_weights(lay)), 0)
 
     def back_hook(i, lay):
@@ -392,11 +453,8 @@
     forward(2, lambda: finish(0))
     loss_grad(2)
 
-    def back_send_1(i, lay):
-        back_full(lay)
-        pl.when(i < 2)(lambda: send_layer(lay, lay - 2))
-
-    lax.fori_loop(0, L, layers(3, back_send_1), 0)
+    lax.fori_loop(0, 2, layers(3, back_send), 0)
+    lax.fori_loop(0, 2, layers(1, lambda i, lay: back_full(lay)), 0)
 
     forward(3)
     loss_grad(3)
@@ -439,7 +497,7 @@
                 pltpu.VMEM((4, 8, 32, 256), F32), pltpu.VMEM((4, 8, 16, 256), F32),
                 pltpu.VMEM((4, 8, 16, 256), F32), pltpu.VMEM((4, 8, 16, 256), F32),
                 pltpu.VMEM((4, 8, 128, 256), F32),
-                dma((26,)), dma((12, 3)), dma((12, 3)), dma((6, 12)), dma((6, 12)),
+                dma((26,)), dma((12, 3)), dma((12, 3)), dma((6, 12)), dma((6, 12)), dma((2, 8)), dma((2, 8)),
             ],
             compiler_params=pltpu.CompilerParams(
                 collective_id=0, has_side_effects=True, vmem_limit_bytes=28 * 2**20),

time: 84 us -> 86.6 us (1.031)
  Pallas kernels: 82.9 us -> 85.6 us
    pallas_call x1, Pallas kernels: 74.4 us -> 77.1 us  [device_fn(): pl.pallas_call(main_body, out_shape=shapes, in_specs=[HBM] * 8, out_specs...]
where the time goes in v3:
time: 86.6 us; the launch traced here: 86.4 us
  Pallas kernels  85.6 us (99%)
    pallas_call x1, Pallas kernels, device_fn(): pl.pallas_call(main_body, out_shape=shapes, in_specs=[HBM] * 8, out_specs...  77.1 us
    pallas_call x1, Pallas kernels, device_fn(): pl.pallas_call(write_body, out_shape=shapes, in_specs=[VMEM] * 6, out_spe...  8.56 us

profile of v3, /device:TPU:0, one launch (start us, length us, event | category | flops | bytes accessed | tf_op | source)
XLA Modules:
  0.0 86.4 jit_solution(11100173243010238584)
XLA Ops:
  0.6 77.1 %diloco_round.1 = (f32[1,4,256,1024]{3,2,1,0:T(8,128)S(1)}, f32[1,4,1024,256]{3,2,1,0:T(8,128)S(1)}, f32[4,256,1024]{2,1,0:T(8,128)S(1)}, f32[4,1024,256]{2,1,0:...) custom-call(f32[1,4,256,1024]{3,2,1,0:T(8,128)} %w1_in.1, f32[1,4,1024,256]{3,2,1,0:T(8,128)} %w2_in.1, ...), custom_call_target="tpu_custom_call" | custom-call | tf_op jit(solution)/shard_map/diloco_round/pallas_call | solution.py:485
  77.7 8.6 %write_out.1 = (f32[1,4,256,1024]{3,2,1,0:T(8,128)}, f32[1,4,1024,256]{3,2,1,0:T(8,128)}, f32[4,256,1024]{2,1,0:T(8,128)}, f32[4,1024,256]{2,1,0:T(8,128)}, f32[...) custom-call(f32[1,4,256,1024]{3,2,1,0:T(8,128)S(1)} %get-tuple-element.12.refs_0_, ...), custom_call_target="tpu_custom_call" | custom-call | tf_op jit(solution)/shard_map/write_out/pallas_call | solution.py:506

commit v4 on v3

--- a/solution.py
+++ b/solution.py
@@ -55,7 +55,7 @@
               w1, w2, g1, g2, m1, m2,
               xb, yb, w1b, w2b, hb, ub, du, hid, dhid, eb, cb,
               delta, raw, s1, r1, s2, r2, full,
-              ld_sem, s0_send, s0_recv, st_send, st_recv, un_send, un_recv):
+              ld_sem, s0_send, s0_recv, st_send, st_recv):
     zc = lax.axis_index('shard')
     wk = lax.axis_index('worker')
     core = lax.rem(wk, 2)
@@ -326,25 +326,10 @@
                 full[p, u, rows, :] = s2[p, u] + r2[p, u]
             stage_copy(AG1, gi).start()
 
-    def unit_copy(second, u):
-        p = LAST
-        d0 = dims_of([c for q, c, u0, nu in GROUPS if q == p and u0 <= u < u0 + nu][0])[0]
-        k0 = coord[d0]
-        off = core * 64 + ((1 - k0) if second else k0) * 32
-        ref = full.at[p, u, pl.ds(pl.multiple_of(off, 16), 32)]
-        return pltpu.make_async_remote_copy(
-            src_ref=ref, dst_ref=ref, send_sem=un_send.at[second, u], recv_sem=un_recv.at[second, u],
-            device_id=partner if second else chip_peer(d0), device_id_type=MESH)
-
     def gather_stage2(p):
         for gi in range(3 * p, 3 * p + 3):
             stage_copy(AG1, gi).wait_recv()
-            if p != LAST:
-                stage_copy(AG2, gi).start()
-            else:
-                _, _, u0, nu = GROUPS[gi]
-                for u in range(u0, u0 + nu):
-                    unit_copy(0, u).start()
+            stage_copy(AG2, gi).start()
             stage_copy(DDA, gi).start()
 
     def gather_stage3(p):
@@ -380,27 +365,13 @@
             outer_unit(frag, p, u)
 
     def finish(frag):
-        load_momentum(frag, LAST)
-        first = [(u0, u0 + nu) for q, c, u0, nu in GROUPS if q == LAST]
-        order = [u0 + i for i in range(3) for u0, end in first if u0 + i < end]
-        for gi in range(3 * LAST, 3 * LAST + 3):
-            stage_copy(DDA, gi).wait_recv()
-        for idx in range(8 + 3):
-            if idx < 8:
-                unit_copy(0, order[idx]).wait_recv()
-                unit_copy(1, order[idx]).start()
-            if idx >= 3:
-                unit_copy(1, order[idx - 3]).wait_recv()
-                outer_unit(frag, LAST, order[idx - 3])
+        gather_stage3(LAST)
+        outer_update(frag, LAST)
         for gi in range(12):
             for cp in rs0_copies(gi):
                 cp.wait_send()
             for stage in range(6):
-                if GROUPS[gi][0] != LAST or stage not in (AG2, DDB):
-                    stage_copy(stage, gi).wait_send()
-        for u in range(8):
-            unit_copy(0, u).wait_send()
-            unit_copy(1, u).wait_send()
+                stage_copy(stage, gi).wait_send()
 
     def sync(frag):
         reduce_stage1(3)
@@ -497,7 +468,7 @@
                 pltpu.VMEM((4, 8, 32, 256), F32), pltpu.VMEM((4, 8, 16, 256), F32),
                 pltpu.VMEM((4, 8, 16, 256), F32), pltpu.VMEM((4, 8, 16, 256), F32),
                 pltpu.VMEM((4, 8, 128, 256), F32),
-                dma((26,)), dma((12, 3)), dma((12, 3)), dma((6, 12)), dma((6, 12)), dma((2, 8)), dma((2, 8)),
+                dma((26,)), dma((12, 3)), dma((12, 3)), dma((6, 12)), dma((6, 12)),
             ],
             compiler_params=pltpu.CompilerParams(
                 collective_id=0, has_side_effects=True, vmem_limit_bytes=28 * 2**20),

time: 86.6 us -> 85.9 us (level)
  no operation moved by 1% of the time
where the time goes in v4:
time: 85.9 us; the launch traced here: 85.8 us
  Pallas kernels  85 us (99%)
    pallas_call x1, Pallas kernels, device_fn(): pl.pallas_call(main_body, out_shape=shapes, in_specs=[HBM] * 8, out_specs...  76.4 us
    pallas_call x1, Pallas kernels, device_fn(): pl.pallas_call(write_body, out_shape=shapes, in_specs=[VMEM] * 6, out_spe...  8.56 us

profile of v4, /device:TPU:0, one launch (start us, length us, event | category | flops | bytes accessed | tf_op | source)
XLA Modules:
  0.0 85.8 jit_solution(8869561618142618706)
XLA Ops:
  0.6 76.4 %diloco_round.1 = (f32[1,4,256,1024]{3,2,1,0:T(8,128)S(1)}, f32[1,4,1024,256]{3,2,1,0:T(8,128)S(1)}, f32[4,256,1024]{2,1,0:T(8,128)S(1)}, f32[4,1024,256]{2,1,0:...) custom-call(f32[1,4,256,1024]{3,2,1,0:T(8,128)} %w1_in.1, f32[1,4,1024,256]{3,2,1,0:T(8,128)} %w2_in.1, ...), custom_call_target="tpu_custom_call" | custom-call | tf_op jit(solution)/shard_map/diloco_round/pallas_call | solution.py:456
  77.0 8.6 %write_out.1 = (f32[1,4,256,1024]{3,2,1,0:T(8,128)}, f32[1,4,1024,256]{3,2,1,0:T(8,128)}, f32[4,256,1024]{2,1,0:T(8,128)}, f32[4,1024,256]{2,1,0:T(8,128)}, f32[...) custom-call(f32[1,4,256,1024]{3,2,1,0:T(8,128)S(1)} %get-tuple-element.12.refs_0_, ...), custom_call_target="tpu_custom_call" | custom-call | tf_op jit(solution)/shard_map/write_out/pallas_call | solution.py:477

commit v5 on v2

--- a/solution.py
+++ b/solution.py
@@ -100,18 +100,10 @@
     x_load = pltpu.make_async_copy(x_in.at[0], xb, ld_sem.at[6 * L])
     y_load = pltpu.make_async_copy(y_in.at[0], yb, ld_sem.at[6 * L + 1])
     x_load.start()
-    for cp in w_load(0):
-        cp.start()
-    y_load.start()
-    for lay in range(1, L):
+    for lay in range(2):
         for cp in w_load(lay):
             cp.start()
-    for lay in range(L):
-        for mat in (1, 2):
-            g_load(mat, lay).start()
-    for lay in range(L):
-        for mat in (1, 2):
-            m_load(mat, lay).start()
+    y_load.start()
     x_load.wait()
     y_load.wait()
 
@@ -183,6 +175,18 @@
         for cp in w_load(lay):
             cp.wait()
 
+        @pl.when(lay == 0)
+        def _():
+            for nxt in range(2, L):
+                for cp in w_load(nxt):
+                    cp.start()
+
+        @pl.when(lay == 1)
+        def _():
+            for nxt in (1, 0):
+                g_load(2, nxt).start()
+                g_load(1, nxt).start()
+
         def cast(i, _):
             rows = pl.ds(pl.multiple_of(i * 64, 64), 64)
             w1b[lay, rows, :] = w1[0, lay, rows, :].astype(BF16)
@@ -361,6 +365,11 @@
                 make_delta(p + 1, lay)
 
     forward(0)
+    for part, mat in PIECES:
+        m_load(mat, part).start()
+    for part, mat in PIECES:
+        g_load(mat, 2 + part).start()
+        m_load(mat, 2 + part).start()
     pl.semaphore_wait(bar, 7)
     loss_grad(0)
     lax.fori_loop(0, 2, layers(3, lambda i, lay: back_chain(lay)), 0)

time: 84 us -> 84.9 us (1.011)
  Pallas kernels: 82.9 us -> 83.8 us
    pallas_call x1, Pallas kernels: 74.4 us -> 75.3 us  [device_fn(): pl.pallas_call(main_body, out_shape=shapes, in_specs=[HBM] * 8, out_specs...]
where the time goes in v5:
time: 84.9 us; the launch traced here: 84.6 us
  Pallas kernels  83.8 us (99%)
    pallas_call x1, Pallas kernels, device_fn(): pl.pallas_call(main_body, out_shape=shapes, in_specs=[HBM] * 8, out_specs...  75.3 us
    pallas_call x1, Pallas kernels, device_fn(): pl.pallas_call(write_body, out_shape=shapes, in_specs=[VMEM] * 6, out_spe...  8.56 us

profile of v5, /device:TPU:0, one launch (start us, length us, event | category | flops | bytes accessed | tf_op | source)
XLA Modules:
  0.0 84.6 jit_solution(11262970836034294556)
XLA Ops:
  0.6 75.3 %diloco_round.1 = (f32[1,4,256,1024]{3,2,1,0:T(8,128)S(1)}, f32[1,4,1024,256]{3,2,1,0:T(8,128)S(1)}, f32[4,256,1024]{2,1,0:T(8,128)S(1)}, f32[4,1024,256]{2,1,0:...) custom-call(f32[1,4,256,1024]{3,2,1,0:T(8,128)} %w1_in.1, f32[1,4,1024,256]{3,2,1,0:T(8,128)} %w2_in.1, ...), custom_call_target="tpu_custom_call" | custom-call | tf_op jit(solution)/shard_map/diloco_round/pallas_call | solution.py:436
  75.9 8.6 %write_out.1 = (f32[1,4,256,1024]{3,2,1,0:T(8,128)}, f32[1,4,1024,256]{3,2,1,0:T(8,128)}, f32[4,256,1024]{2,1,0:T(8,128)}, f32[4,1024,256]{2,1,0:T(8,128)}, f32[...) custom-call(f32[1,4,256,1024]{3,2,1,0:T(8,128)S(1)} %get-tuple-element.12.refs_0_, ...), custom_call_target="tpu_custom_call" | custom-call | tf_op jit(solution)/shard_map/write_out/pallas_call | solution.py:457

commit v6 on v4

--- a/solution.py
+++ b/solution.py
@@ -32,7 +32,6 @@
         GROUPS.append((piece_idx, color, first_unit, COLOR_UNITS[piece_idx][color]))
         first_unit += COLOR_UNITS[piece_idx][color]
 GATHER_ORDER = (0, 2, 3, 1)
-LAST = GATHER_ORDER[-1]
 RS1, X2, AG1, AG2, DDA, DDB = range(6)
 
 
@@ -51,10 +50,16 @@
     return u, du
 
 
+def unit_slice(mat, u):
+    if mat == 2:
+        return pl.ds(u * 128, 128), pl.ds(0, 256)
+    return pl.ds((u % 2) * 128, 128), pl.ds((u // 2) * 256, 256)
+
+
 def main_body(w1_in, w2_in, g1_in, g2_in, m1_in, m2_in, x_in, y_in,
-              w1, w2, g1, g2, m1, m2,
+              w1, w2, g1, g2, m1, m2, full,
               xb, yb, w1b, w2b, hb, ub, du, hid, dhid, eb, cb,
-              delta, raw, s1, r1, s2, r2, full,
+              delta, raw, s1, r1, s2, r2,
               ld_sem, s0_send, s0_recv, st_send, st_recv):
     zc = lax.axis_index('shard')
     wk = lax.axis_index('worker')
@@ -114,6 +119,7 @@
         for mat in (1, 2):
             m_load(mat, lay).start()
     x_load.wait()
+    y_load.wait()
 
     def dims_of(color_idx):
         return color_idx % 3, (color_idx + 1) % 3, (color_idx + 2) % 3
@@ -163,37 +169,13 @@
             src_ref=src, dst_ref=dst, send_sem=st_send.at[stage, gi], recv_sem=st_recv.at[stage, gi],
             device_id=dev, device_id_type=MESH)
 
-    def unit_slice(mat, u):
-        if mat == 2:
-            return pl.ds(u * 128, 128), pl.ds(0, 256)
-        return pl.ds((u % 2) * 128, 128), pl.ds((u // 2) * 256, 256)
-
-    def layer_0(lay, _):
-        load1, load2 = w_load(lay)
-        h_bf = hid[...].astype(BF16)
-        hb[lay] = h_bf
-        load1.wait()
-        for j in range(NB):
-            cols = slice(j * D, (j + 1) * D)
-            w_bf = w1[0, lay, :, cols].astype(BF16)
-            w1b[lay, :, cols] = w_bf
-            u, dg = gelu_pair(dot(h_bf, w_bf, 1, 0))
-            ub[lay, :, cols] = u.astype(BF16)
-            du[lay, :, cols] = dg
-        load2.wait()
-        acc = hid[...]
-        for j in range(NB):
-            cols = slice(j * D, (j + 1) * D)
-            w_bf = w2[0, lay, cols, :].astype(BF16)
-            w2b[lay, cols, :] = w_bf
-            acc = acc + dot(ub[lay, :, cols], w_bf, 1, 0)
-        hid[...] = acc
-        return 0
-
     def forward(k, before_layer_1=None):
         hid[...] = xb[k].astype(F32)
 
         def layer(lay, _):
+            if k == 0:
+                for cp in w_load(lay):
+                    cp.wait()
             if before_layer_1 is not None:
                 pl.when(lay == 1)(before_layer_1)
             h_bf = hid[...].astype(BF16)
@@ -201,6 +183,9 @@
             acc = hid[...]
             for j in range(NB):
                 cols = slice(j * D, (j + 1) * D)
+                if k == 0:
+                    w1b[lay, :, cols] = w1[0, lay, :, cols].astype(BF16)
+                    w2b[lay, cols, :] = w2[0, lay, cols, :].astype(BF16)
                 a = dot(h_bf, w1b[lay, :, cols], 1, 0)
                 u, dg = gelu_pair(a)
                 u_bf = u.astype(BF16)
@@ -210,7 +195,7 @@
             hid[...] = acc
             return 0
 
-        lax.fori_loop(0, L, layer_0 if k == 0 else layer, 0)
+        lax.fori_loop(0, L, layer, 0)
 
     def loss_grad(k):
         dhid[...] = (2.0 / (B * D)) * (hid[...] - yb[k].astype(F32))
@@ -337,36 +322,37 @@
             stage_copy(AG2, gi).wait_recv()
             stage_copy(DDB, gi).start()
 
-    def outer_unit(frag, p, u):
+    def outer_update(frag, p):
         part, mat = PIECES[p]
         lay = 2 * frag + part
         wr, wbr, gr, mr = (w1, w1b, g1, m1) if mat == 1 else (w2, w2b, g2, m2)
-        rows, cols = unit_slice(mat, u)
-        mean = full[p, u] * (1.0 / N_ALL)
-        mom = OUTER_MOM * mr[lay, rows, cols] + mean
-        glob = gr[lay, rows, cols] - OUTER_LR * (OUTER_MOM * mom + mean)
-        mr[lay, rows, cols] = mom
-        gr[lay, rows, cols] = glob
-        merged = MERGE_MIX * wr[0, lay, rows, cols] + (1.0 - MERGE_MIX) * glob
-        wr[0, lay, rows, cols] = merged
-        if frag == 0:
+        m_load(mat, lay).wait()
+        wait_gathered(p)
+        for u in range(8):
+            rows, cols = unit_slice(mat, u)
+            mean = full[p, u] * (1.0 / N_ALL)
+            mom = OUTER_MOM * mr[lay, rows, cols] + mean
+            glob = gr[lay, rows, cols] - OUTER_LR * (OUTER_MOM * mom + mean)
+            mr[lay, rows, cols] = mom
+            gr[lay, rows, cols] = glob
+            merged = MERGE_MIX * wr[0, lay, rows, cols] + (1.0 - MERGE_MIX) * glob
+            wr[0, lay, rows, cols] = merged
             wbr[lay, rows, cols] = merged.astype(BF16)
 
-    def load_momentum(frag, p):
-        part, mat = PIECES[p]
-        m_load(mat, 2 * frag + part).wait()
-
-    def outer_update(frag, p):
-        load_momentum(frag, p)
+    last_piece = GATHER_ORDER[-1]
+
+    def wait_gathered(p):
         for gi in range(3 * p, 3 * p + 3):
             stage_copy(DDA, gi).wait_recv()
             stage_copy(DDB, gi).wait_recv()
-        for u in range(8):
-            outer_unit(frag, p, u)
 
     def finish(frag):
-        gather_stage3(LAST)
-        outer_update(frag, LAST)
+        if frag == 0:
+            outer_update(frag, last_piece)
+        else:
+            for p, (part, mat) in enumerate(PIECES):
+                m_load(mat, 2 + part).wait()
+                wait_gathered(p)
         for gi in range(12):
             for cp in rs0_copies(gi):
                 cp.wait_send()
@@ -382,12 +368,11 @@
         for p in GATHER_ORDER:
             gather_stage2(p)
         prev = None
-        for p in GATHER_ORDER[:-1]:
+        for p in GATHER_ORDER:
             gather_stage3(p)
-            if prev is not None:
+            if prev is not None and frag == 0:
                 outer_update(frag, prev)
             prev = p
-        outer_update(frag, prev)
 
     def layers(lo, body):
         def run(i, _):
@@ -396,7 +381,6 @@
         return run
 
     forward(0)
-    y_load.wait()
     pl.semaphore_wait(bar, 7)
     loss_grad(0)
     lax.fori_loop(0, 2, layers(3, lambda i, lay: back_chain(lay)), 0)
@@ -434,16 +418,35 @@
     finish(1)
 
 
-def write_body(*refs):
-    srcs, dsts, sem = refs[:6], refs[6:12], refs[12]
+def write_body(w1, w2, g1, g2, m1, m2, full, *refs):
+    dsts, stages, sem = refs[:6], refs[6:12], refs[12]
+    srcs = (w1, w2, g1, g2, m1, m2)
     cps = []
-    for i in range(6):
-        for lay in range(L):
-            src = srcs[i].at[0, lay] if i < 2 else srcs[i].at[lay]
-            dst = dsts[i].at[0, lay] if i < 2 else dsts[i].at[lay]
-            cps.append(pltpu.make_async_copy(src, dst, sem.at[i, lay]))
-    for cp in cps:
+
+    def put(src, i, lay):
+        dst = dsts[i].at[0, lay] if i < 2 else dsts[i].at[lay]
+        cp = pltpu.make_async_copy(src, dst, sem.at[i, lay])
         cp.start()
+        cps.append(cp)
+
+    for lay in range(2):
+        for i in range(6):
+            put(srcs[i].at[0, lay] if i < 2 else srcs[i].at[lay], i, lay)
+    for p, (part, mat) in enumerate(PIECES):
+        lay = 2 + part
+        k = mat - 1
+        wr, gr, mr = srcs[k], srcs[2 + k], srcs[4 + k]
+        ws, gs, ms = stages[k], stages[2 + k], stages[4 + k]
+        for u in range(8):
+            rows, cols = unit_slice(mat, u)
+            mean = full[p, u] * (1.0 / N_ALL)
+            mom = OUTER_MOM * mr[lay, rows, cols] + mean
+            glob = gr[lay, rows, cols] - OUTER_LR * (OUTER_MOM * mom + mean)
+            ms[part, rows, cols] = mom
+            gs[part, rows, cols] = glob
+            ws[part, rows, cols] = MERGE_MIX * wr[0, lay, rows, cols] + (1.0 - MERGE_MIX) * glob
+        for idx, st in enumerate((ws, gs, ms)):
+            put(st.at[part], 2 * idx + k, lay)
     for cp in cps:
         cp.wait()
 
@@ -455,9 +458,9 @@
         dma = pltpu.SemaphoreType.DMA
         work = pl.pallas_call(
             main_body,
-            out_shape=shapes,
+            out_shape=shapes + [jax.ShapeDtypeStruct((4, 8, 128, 256), F32)],
             in_specs=[HBM] * 8,
-            out_specs=[VMEM] * 6,
+            out_specs=[VMEM] * 7,
             scratch_shapes=[
                 pltpu.VMEM((H, B, D), BF16), pltpu.VMEM((H, B, D), BF16),
                 pltpu.VMEM((L, D, FF), BF16), pltpu.VMEM((L, FF, D), BF16),
@@ -467,20 +470,19 @@
                 pltpu.VMEM((4, 8, 128, 256), BF16), pltpu.VMEM((3, 4, 8, 32, 256), BF16),
                 pltpu.VMEM((4, 8, 32, 256), F32), pltpu.VMEM((4, 8, 16, 256), F32),
                 pltpu.VMEM((4, 8, 16, 256), F32), pltpu.VMEM((4, 8, 16, 256), F32),
-                pltpu.VMEM((4, 8, 128, 256), F32),
                 dma((26,)), dma((12, 3)), dma((12, 3)), dma((6, 12)), dma((6, 12)),
             ],
             compiler_params=pltpu.CompilerParams(
-                collective_id=0, has_side_effects=True, vmem_limit_bytes=28 * 2**20),
+                collective_id=0, has_side_effects=True, vmem_limit_bytes=22 * 2**20),
             name='diloco_round',
         )(*[pltpu.with_memory_space_constraint(a, pltpu.HBM) for a in (*arrays, x_loc, y_loc)])
         outs = pl.pallas_call(
             write_body,
             out_shape=shapes,
-            in_specs=[VMEM] * 6,
+            in_specs=[VMEM] * 7,
             out_specs=[HBM] * 6,
-            scratch_shapes=[dma((6, L))],
-            compiler_params=pltpu.CompilerParams(vmem_limit_bytes=2 * 2**20),
+            scratch_shapes=[pltpu.VMEM((2, D, FF), F32), pltpu.VMEM((2, FF, D), F32)] * 3 + [dma((6, L))],
+            compiler_params=pltpu.CompilerParams(vmem_limit_bytes=16 * 2**20),
             name='write_out',
         )(*work)
         return tuple(outs)

time: 85.9 us -> 83.5 us (0.972)
  Pallas kernels: 85 us -> 82.6 us
    pallas_call x2, Pallas kernels: 85 us -> 82.6 us  [the longest x1 74 us: device_fn(): pl.pallas_call(main_body, out_shape=shapes + [jax.ShapeDtypeStruct((4, 8,...]
where the time goes in v6:
time: 83.5 us; the launch traced here: 83.4 us
  Pallas kernels  82.6 us (99%)
    pallas_call x1, Pallas kernels, device_fn(): pl.pallas_call(main_body, out_shape=shapes + [jax.ShapeDtypeStruct((4, 8,...  74 us
    pallas_call x1, Pallas kernels, device_fn(): pl.pallas_call(write_body, out_shape=shapes, in_specs=[VMEM] * 7, out_spe...  8.56 us

profile of v6, /device:TPU:0, one launch (start us, length us, event | category | flops | bytes accessed | tf_op | source)
XLA Modules:
  0.0 83.4 jit_solution(2078355429942859677)
XLA Ops:
  0.6 74.0 %diloco_round.1 = (f32[1,4,256,1024]{3,2,1,0:T(8,128)S(1)}, f32[1,4,1024,256]{3,2,1,0:T(8,128)S(1)}, f32[4,256,1024]{2,1,0:T(8,128)S(1)}, f32[4,1024,256]{2,1,0:...) custom-call(f32[1,4,256,1024]{3,2,1,0:T(8,128)} %w1_in.1, ...), custom_call_target="tpu_custom_call" | custom-call | tf_op jit(solution)/shard_map/diloco_round/pallas_call | solution.py:459
  74.6 8.6 %write_out.1 = (f32[1,4,256,1024]{3,2,1,0:T(8,128)}, f32[1,4,1024,256]{3,2,1,0:T(8,128)}, f32[4,256,1024]{2,1,0:T(8,128)}, f32[4,1024,256]{2,1,0:T(8,128)}, f32[...) custom-call(f32[1,4,256,1024]{3,2,1,0:T(8,128)S(1)} %get-tuple-element.13.w1, f32[1,4,1024,256]{3,2,1,0:T(8,128)S(1)} %get-tuple-element.14.w2, ...), custom_call_target="tpu_custom_call" | custom-call | tf_op jit(solution)/shard_map/write_out/pallas_call | solution.py:479

commit v7 on v6

--- a/solution.py
+++ b/solution.py
@@ -360,7 +360,6 @@
                 stage_copy(stage, gi).wait_send()
 
     def sync(frag):
-        reduce_stage1(3)
         for p in range(4):
             reduce_stage2(p)
         for p in range(4):
@@ -391,17 +390,14 @@
     def back_hook(i, lay):
         back_full(lay)
 
-        @pl.when(i == 0)
-        def _():
-            reduce_stage1(0)
-            reduce_stage1(1)
-
-        @pl.when(i == 2)
-        def _():
-            reduce_stage1(2)
+        for p in range(1, 4):
+            @pl.when(i == p - 1)
+            def _(p=p):
+                reduce_stage1(p)
 
     forward(1)
     loss_grad(1)
+    reduce_stage1(0)
     lax.fori_loop(0, L, layers(3, back_hook), 0)
     sync(0)
 
@@ -413,6 +409,7 @@
 
     forward(3)
     loss_grad(3)
+    reduce_stage1(0)
     lax.fori_loop(0, L, layers(3, back_hook), 0)
     sync(1)
     finish(1)

time: 83.5 us -> 82.7 us (level)
  Pallas kernels: 82.6 us -> 81.7 us
where the time goes in v7:
time: 82.7 us; the launch traced here: 82.5 us
  Pallas kernels  81.7 us (99%)
    pallas_call x1, Pallas kernels, device_fn(): pl.pallas_call(main_body, out_shape=shapes + [jax.ShapeDtypeStruct((4, 8,...  73.2 us
    pallas_call x1, Pallas kernels, device_fn(): pl.pallas_call(write_body, out_shape=shapes, in_specs=[VMEM] * 7, out_spe...  8.56 us

profile of v7, /device:TPU:0, one launch (start us, length us, event | category | flops | bytes accessed | tf_op | source)
XLA Modules:
  0.0 82.5 jit_solution(10032155073842531362)
XLA Ops:
  0.6 73.2 %diloco_round.1 = (f32[1,4,256,1024]{3,2,1,0:T(8,128)S(1)}, f32[1,4,1024,256]{3,2,1,0:T(8,128)S(1)}, f32[4,256,1024]{2,1,0:T(8,128)S(1)}, f32[4,1024,256]{2,1,0:...) custom-call(f32[1,4,256,1024]{3,2,1,0:T(8,128)} %w1_in.1, ...), custom_call_target="tpu_custom_call" | custom-call | tf_op jit(solution)/shard_map/diloco_round/pallas_call | solution.py:456
  73.8 8.6 %write_out.1 = (f32[1,4,256,1024]{3,2,1,0:T(8,128)}, f32[1,4,1024,256]{3,2,1,0:T(8,128)}, f32[4,256,1024]{2,1,0:T(8,128)}, f32[4,1024,256]{2,1,0:T(8,128)}, f32[...) custom-call(f32[1,4,256,1024]{3,2,1,0:T(8,128)S(1)} %get-tuple-element.13.w1, f32[1,4,1024,256]{3,2,1,0:T(8,128)S(1)} %get-tuple-element.14.w2, ...), custom_call_target="tpu_custom_call" | custom-call | tf_op jit(solution)/shard_map/write_out/pallas_call | solution.py:476

commit v8 on v7

--- a/solution.py
+++ b/solution.py
@@ -218,7 +218,7 @@
                     for cp in rs0_copies(gi):
                         cp.start()
 
-    def back_send(i, lay):
+    def back_send(i, lay, after_first=None):
         p = 2 * i
         e = dhid[...].astype(BF16)
         h_bf = hb[lay]
@@ -231,6 +231,8 @@
             delta[p, 2 * j] = dl[:128]
             delta[p, 2 * j + 1] = dl[128:]
         send_piece(i, 0)
+        if after_first is not None:
+            pl.when(i == 0)(after_first)
         g_load(1, lay).wait()
         acc = dhid[...]
         for j in range(NB):
@@ -248,7 +250,7 @@
         send_piece(i, 1)
         w2b[lay] = w2[0, lay].astype(BF16)
 
-    def back_full(lay):
+    def back_full(lay, need_input_grad=True):
         e = dhid[...].astype(BF16)
         h_bf = hb[lay]
         acc = dhid[...]
@@ -257,9 +259,11 @@
             d_u = dot(e, w2b[lay, cols, :], 1, 1)
             c = (du[lay, :, cols] * d_u).astype(BF16)
             update2(lay, cols, ub[lay, :, cols], e)
-            acc = acc + dot(c, w1b[lay, :, cols], 1, 1)
+            if need_input_grad:
+                acc = acc + dot(c, w1b[lay, :, cols], 1, 1)
             update1(lay, cols, h_bf, c)
-        dhid[...] = acc
+        if need_input_grad:
+            dhid[...] = acc
 
     def back_chain(lay):
         e = dhid[...].astype(BF16)
@@ -322,22 +326,24 @@
             stage_copy(AG2, gi).wait_recv()
             stage_copy(DDB, gi).start()
 
-    def outer_update(frag, p):
-        part, mat = PIECES[p]
-        lay = 2 * frag + part
+    def outer_update(p, merge=True, outer=True):
+        lay, mat = PIECES[p]
         wr, wbr, gr, mr = (w1, w1b, g1, m1) if mat == 1 else (w2, w2b, g2, m2)
-        m_load(mat, lay).wait()
-        wait_gathered(p)
+        if merge:
+            m_load(mat, lay).wait()
+            wait_gathered(p)
         for u in range(8):
             rows, cols = unit_slice(mat, u)
             mean = full[p, u] * (1.0 / N_ALL)
             mom = OUTER_MOM * mr[lay, rows, cols] + mean
             glob = gr[lay, rows, cols] - OUTER_LR * (OUTER_MOM * mom + mean)
-            mr[lay, rows, cols] = mom
-            gr[lay, rows, cols] = glob
-            merged = MERGE_MIX * wr[0, lay, rows, cols] + (1.0 - MERGE_MIX) * glob
-            wr[0, lay, rows, cols] = merged
-            wbr[lay, rows, cols] = merged.astype(BF16)
+            if outer:
+                mr[lay, rows, cols] = mom
+                gr[lay, rows, cols] = glob
+            if merge:
+                merged = MERGE_MIX * wr[0, lay, rows, cols] + (1.0 - MERGE_MIX) * glob
+                wr[0, lay, rows, cols] = merged
+                wbr[lay, rows, cols] = merged.astype(BF16)
 
     last_piece = GATHER_ORDER[-1]
 
@@ -348,7 +354,7 @@
 
     def finish(frag):
         if frag == 0:
-            outer_update(frag, last_piece)
+            outer_update(last_piece, outer=False)
         else:
             for p, (part, mat) in enumerate(PIECES):
                 m_load(mat, 2 + part).wait()
@@ -370,7 +376,7 @@
         for p in GATHER_ORDER:
             gather_stage3(p)
             if prev is not None and frag == 0:
-                outer_update(frag, prev)
+                outer_update(prev)
             prev = p
 
     def layers(lo, body):
@@ -398,19 +404,23 @@
     forward(1)
     loss_grad(1)
     reduce_stage1(0)
-    lax.fori_loop(0, L, layers(3, back_hook), 0)
+    lax.fori_loop(0, 3, layers(3, back_hook), 0)
+    back_full(0, False)
     sync(0)
 
     forward(2, lambda: finish(0))
     loss_grad(2)
 
-    lax.fori_loop(0, 2, layers(3, back_send), 0)
-    lax.fori_loop(0, 2, layers(1, lambda i, lay: back_full(lay)), 0)
+    lax.fori_loop(0, 2, layers(3, lambda i, lay: back_send(
+        i, lay, lambda: outer_update(last_piece, merge=False))), 0)
+    back_full(1)
+    back_full(0, False)
 
     forward(3)
     loss_grad(3)
     reduce_stage1(0)
-    lax.fori_loop(0, L, layers(3, back_hook), 0)
+    lax.fori_loop(0, 3, layers(3, back_hook), 0)
+    back_full(0, False)
     sync(1)
     finish(1)
 

time: 82.7 us -> 82.2 us (level)
  no operation moved by 1% of the time
where the time goes in v8:
time: 82.2 us; the launch traced here: 82.1 us
  Pallas kernels  81.3 us (99%)
    pallas_call x1, Pallas kernels, device_fn(): pl.pallas_call(main_body, out_shape=shapes + [jax.ShapeDtypeStruct((4, 8,...  72.7 us
    pallas_call x1, Pallas kernels, device_fn(): pl.pallas_call(write_body, out_shape=shapes, in_specs=[VMEM] * 7, out_spe...  8.56 us

profile of v8, /device:TPU:0, one launch (start us, length us, event | category | flops | bytes accessed | tf_op | source)
XLA Modules:
  0.0 82.1 jit_solution(4552004890417475535)
XLA Ops:
  0.6 72.7 %diloco_round.1 = (f32[1,4,256,1024]{3,2,1,0:T(8,128)S(1)}, f32[1,4,1024,256]{3,2,1,0:T(8,128)S(1)}, f32[4,256,1024]{2,1,0:T(8,128)S(1)}, f32[4,1024,256]{2,1,0:...) custom-call(f32[1,4,256,1024]{3,2,1,0:T(8,128)} %w1_in.1, ...), custom_call_target="tpu_custom_call" | custom-call | tf_op jit(solution)/shard_map/diloco_round/pallas_call | solution.py:466
  73.4 8.6 %write_out.1 = (f32[1,4,256,1024]{3,2,1,0:T(8,128)}, f32[1,4,1024,256]{3,2,1,0:T(8,128)}, f32[4,256,1024]{2,1,0:T(8,128)}, f32[4,1024,256]{2,1,0:T(8,128)}, f32[...) custom-call(f32[1,4,256,1024]{3,2,1,0:T(8,128)S(1)} %get-tuple-element.13.w1, f32[1,4,1024,256]{3,2,1,0:T(8,128)S(1)} %get-tuple-element.14.w2, ...), custom_call_target="tpu_custom_call" | custom-call | tf_op jit(solution)/shard_map/write_out/pallas_call | solution.py:486

commit v9 on v8

--- a/solution.py
+++ b/solution.py
@@ -93,6 +93,12 @@
         return (pltpu.make_async_copy(w1_in.at[0, lay], w1.at[0, lay], ld_sem.at[lay]),
                 pltpu.make_async_copy(w2_in.at[0, lay], w2.at[0, lay], ld_sem.at[L + lay]))
 
+    def w_start(lay):
+        for i in range(4):
+            for src, dst, n, idx in ((w1_in, w1, D // 4, lay), (w2_in, w2, FF // 4, L + lay)):
+                rows = pl.ds(i * n, n)
+                pltpu.make_async_copy(src.at[0, lay, rows], dst.at[0, lay, rows], ld_sem.at[idx]).start()
+
     def g_load(mat, lay):
         if mat == 1:
             return pltpu.make_async_copy(g1_in.at[lay], g1.at[lay], ld_sem.at[2 * L + lay])
@@ -106,12 +112,10 @@
     x_load = pltpu.make_async_copy(x_in.at[0], xb, ld_sem.at[6 * L])
     y_load = pltpu.make_async_copy(y_in.at[0], yb, ld_sem.at[6 * L + 1])
     x_load.start()
-    for cp in w_load(0):
-        cp.start()
+    w_start(0)
     y_load.start()
     for lay in range(1, L):
-        for cp in w_load(lay):
-            cp.start()
+        w_start(lay)
     for lay in range(L):
         for mat in (1, 2):
             g_load(mat, lay).start()
@@ -176,8 +180,8 @@
             if k == 0:
                 for cp in w_load(lay):
                     cp.wait()
-            if before_layer_1 is not None:
-                pl.when(lay == 1)(before_layer_1)
+            if before_layer_1 is not None and lay == 1:
+                before_layer_1()
             h_bf = hid[...].astype(BF16)
             hb[lay] = h_bf
             acc = hid[...]
@@ -195,7 +199,8 @@
             hid[...] = acc
             return 0
 
-        lax.fori_loop(0, L, layer, 0)
+        for lay in range(L):
+            layer(lay, 0)
 
     def loss_grad(k):
         dhid[...] = (2.0 / (B * D)) * (hid[...] - yb[k].astype(F32))
@@ -388,7 +393,8 @@
     forward(0)
     pl.semaphore_wait(bar, 7)
     loss_grad(0)
-    lax.fori_loop(0, 2, layers(3, lambda i, lay: back_chain(lay)), 0)
+    back_chain(3)
+    back_chain(2)
 
     lax.fori_loop(0, 2, layers(1, back_send), 0)
     lax.fori_loop(0, 2, layers(3, lambda i, lay: back_weights(lay)), 0)
@@ -432,9 +438,10 @@
 
     def put(src, i, lay):
         dst = dsts[i].at[0, lay] if i < 2 else dsts[i].at[lay]
-        cp = pltpu.make_async_copy(src, dst, sem.at[i, lay])
-        cp.start()
-        cps.append(cp)
+        half = src.shape[0] // 2
+        for rows in (pl.ds(0, half), pl.ds(half, half)):
+            pltpu.make_async_copy(src.at[rows], dst.at[rows], sem.at[i, lay]).start()
+        cps.append(pltpu.make_async_copy(src, dst, sem.at[i, lay]))
 
     for lay in range(2):
         for i in range(6):

time: 82.2 us -> 81.9 us (level)
  no operation moved by 1% of the time
where the time goes in v9:
time: 81.9 us; the launch traced here: 81.8 us
  Pallas kernels  80.9 us (99%)
  between operations  0.82 us (1%)
    pallas_call x1, Pallas kernels, device_fn(): pl.pallas_call(main_body, out_shape=shapes + [jax.ShapeDtypeStruct((4, 8,...  72.4 us
    pallas_call x1, Pallas kernels, device_fn(): pl.pallas_call(write_body, out_shape=shapes, in_specs=[VMEM] * 7, out_spe...  8.53 us

profile of v9, /device:TPU:0, one launch (start us, length us, event | category | flops | bytes accessed | tf_op | source)
XLA Modules:
  0.0 81.8 jit_solution(3254612903680242482)
XLA Ops:
  0.6 72.4 %diloco_round.1 = (f32[1,4,256,1024]{3,2,1,0:T(8,128)S(1)}, f32[1,4,1024,256]{3,2,1,0:T(8,128)S(1)}, f32[4,256,1024]{2,1,0:T(8,128)S(1)}, f32[4,1024,256]{2,1,0:...) custom-call(f32[1,4,256,1024]{3,2,1,0:T(8,128)} %w1_in.1, ...), custom_call_target="tpu_custom_call" | custom-call | tf_op jit(solution)/shard_map/diloco_round/pallas_call | solution.py:473
  73.0 8.5 %write_out.1 = (f32[1,4,256,1024]{3,2,1,0:T(8,128)}, f32[1,4,1024,256]{3,2,1,0:T(8,128)}, f32[4,256,1024]{2,1,0:T(8,128)}, f32[4,1024,256]{2,1,0:T(8,128)}, f32[...) custom-call(f32[1,4,256,1024]{3,2,1,0:T(8,128)S(1)} %get-tuple-element.13.w1, f32[1,4,1024,256]{3,2,1,0:T(8,128)S(1)} %get-tuple-element.14.w2, ...), custom_call_target="tpu_custom_call" | custom-call | tf_op jit(solution)/shard_map/write_out/pallas_call | solution.py:493

commit v10 on v9

--- a/solution.py
+++ b/solution.py
@@ -32,7 +32,8 @@
         GROUPS.append((piece_idx, color, first_unit, COLOR_UNITS[piece_idx][color]))
         first_unit += COLOR_UNITS[piece_idx][color]
 GATHER_ORDER = (0, 2, 3, 1)
-RS1, X2, AG1, AG2, DDA, DDB = range(6)
+LAST = GATHER_ORDER[-1]
+RS1, X2, AG1, AG2, DDA, DDB, XOWN, XPART = range(8)
 
 
 def dot(a, b, ca, cb):
@@ -153,6 +154,10 @@
         d0, d1, d2 = dims_of(c)
         k0, k1, k2 = coord[d0], coord[d1], coord[d2]
         us = pl.ds(u0, nu)
+        if p == LAST and stage in (AG2, DDB):
+            us = pl.ds(u0, nu - 1)
+        elif stage in (XOWN, XPART):
+            us = pl.ds(u0 + nu - 1, 1)
         if stage == RS1:
             src, dst, dev = s1.at[p, us, pl.ds(pl.multiple_of((1 - k1) * 16, 16), 16)], r1.at[p, us], chip_peer(d1)
         elif stage == X2:
@@ -161,8 +166,10 @@
             base = core * 64
             if stage == AG1:
                 off, n, dev = base + k0 * 32 + k1 * 16, 16, chip_peer(d1)
-            elif stage == AG2:
+            elif stage in (AG2, XOWN):
                 off, n, dev = base + k0 * 32, 32, chip_peer(d0)
+            elif stage == XPART:
+                off, n, dev = (1 - core) * 64 + k0 * 32, 32, chip_peer(d0)
             elif stage == DDA:
                 off, n, dev = base + k0 * 32, 32, partner
             else:
@@ -324,7 +331,13 @@
         for gi in range(3 * p, 3 * p + 3):
             stage_copy(AG1, gi).wait_recv()
             stage_copy(AG2, gi).start()
+            if p == LAST:
+                stage_copy(XOWN, gi).start()
             stage_copy(DDA, gi).start()
+        if p == LAST:
+            for gi in range(3 * p, 3 * p + 3):
+                stage_copy(DDA, gi).wait_recv()
+                stage_copy(XPART, gi).start()
 
     def gather_stage3(p):
         for gi in range(3 * p, 3 * p + 3):
@@ -350,16 +363,15 @@
                 wr[0, lay, rows, cols] = merged
                 wbr[lay, rows, cols] = merged.astype(BF16)
 
-    last_piece = GATHER_ORDER[-1]
-
     def wait_gathered(p):
         for gi in range(3 * p, 3 * p + 3):
-            stage_copy(DDA, gi).wait_recv()
             stage_copy(DDB, gi).wait_recv()
+            for stage in (XOWN, XPART) if p == LAST else (DDA,):
+                stage_copy(stage, gi).wait_recv()
 
     def finish(frag):
         if frag == 0:
-            outer_update(last_piece, outer=False)
+            outer_update(LAST, outer=False)
         else:
             for p, (part, mat) in enumerate(PIECES):
                 m_load(mat, 2 + part).wait()
@@ -367,7 +379,7 @@
         for gi in range(12):
             for cp in rs0_copies(gi):
                 cp.wait_send()
-            for stage in range(6):
+            for stage in range(8 if GROUPS[gi][0] == LAST else 6):
                 stage_copy(stage, gi).wait_send()
 
     def sync(frag):
@@ -418,7 +430,7 @@
     loss_grad(2)
 
     lax.fori_loop(0, 2, layers(3, lambda i, lay: back_send(
-        i, lay, lambda: outer_update(last_piece, merge=False))), 0)
+        i, lay, lambda: outer_update(LAST, merge=False))), 0)
     back_full(1)
     back_full(0, False)
 
@@ -484,7 +496,7 @@
                 pltpu.VMEM((4, 8, 128, 256), BF16), pltpu.VMEM((3, 4, 8, 32, 256), BF16),
                 pltpu.VMEM((4, 8, 32, 256), F32), pltpu.VMEM((4, 8, 16, 256), F32),
                 pltpu.VMEM((4, 8, 16, 256), F32), pltpu.VMEM((4, 8, 16, 256), F32),
-                dma((26,)), dma((12, 3)), dma((12, 3)), dma((6, 12)), dma((6, 12)),
+                dma((26,)), dma((12, 3)), dma((12, 3)), dma((8, 12)), dma((8, 12)),
             ],
             compiler_params=pltpu.CompilerParams(
                 collective_id=0, has_side_effects=True, vmem_limit_bytes=22 * 2**20),

time: 81.9 us -> 82.2 us (level)
  no operation moved by 1% of the time
where the time goes in v10:
time: 82.2 us; the launch traced here: 82.1 us
  Pallas kernels  81.2 us (99%)
    pallas_call x1, Pallas kernels, device_fn(): pl.pallas_call(main_body, out_shape=shapes + [jax.ShapeDtypeStruct((4, 8,...  72.7 us
    pallas_call x1, Pallas kernels, device_fn(): pl.pallas_call(write_body, out_shape=shapes, in_specs=[VMEM] * 7, out_spe...  8.53 us

profile of v10, /device:TPU:0, one launch (start us, length us, event | category | flops | bytes accessed | tf_op | source)
XLA Modules:
  0.0 82.1 jit_solution(11618993660116293742)
XLA Ops:
  0.6 72.7 %diloco_round.1 = (f32[1,4,256,1024]{3,2,1,0:T(8,128)S(1)}, f32[1,4,1024,256]{3,2,1,0:T(8,128)S(1)}, f32[4,256,1024]{2,1,0:T(8,128)S(1)}, f32[4,1024,256]{2,1,0:...) custom-call(f32[1,4,256,1024]{3,2,1,0:T(8,128)} %w1_in.1, ...), custom_call_target="tpu_custom_call" | custom-call | tf_op jit(solution)/shard_map/diloco_round/pallas_call | solution.py:485
  73.4 8.5 %write_out.1 = (f32[1,4,256,1024]{3,2,1,0:T(8,128)}, f32[1,4,1024,256]{3,2,1,0:T(8,128)}, f32[4,256,1024]{2,1,0:T(8,128)}, f32[4,1024,256]{2,1,0:T(8,128)}, f32[...) custom-call(f32[1,4,256,1024]{3,2,1,0:T(8,128)S(1)} %get-tuple-element.13.w1, f32[1,4,1024,256]{3,2,1,0:T(8,128)S(1)} %get-tuple-element.14.w2, ...), custom_call_target="tpu_custom_call" | custom-call | tf_op jit(solution)/shard_map/write_out/pallas_call | solution.py:505

commit v11 on v9

--- a/solution.py
+++ b/solution.py
@@ -371,12 +371,15 @@
                 stage_copy(stage, gi).wait_send()
 
     def sync(frag):
+        reduce_stage1(3)
         for p in range(4):
             reduce_stage2(p)
         for p in range(4):
             reduce_stage3(p)
         for p in GATHER_ORDER:
             gather_stage2(p)
+        back_full(1)
+        back_full(0, False)
         prev = None
         for p in GATHER_ORDER:
             gather_stage3(p)
@@ -401,8 +404,7 @@
 
     def back_hook(i, lay):
         back_full(lay)
-
-        for p in range(1, 4):
+        for p in (1, 2):
             @pl.when(i == p - 1)
             def _(p=p):
                 reduce_stage1(p)
@@ -410,8 +412,7 @@
     forward(1)
     loss_grad(1)
     reduce_stage1(0)
-    lax.fori_loop(0, 3, layers(3, back_hook), 0)
-    back_full(0, False)
+    lax.fori_loop(0, 2, layers(3, back_hook), 0)
     sync(0)
 
     forward(2, lambda: finish(0))
@@ -425,8 +426,7 @@
     forward(3)
     loss_grad(3)
     reduce_stage1(0)
-    lax.fori_loop(0, 3, layers(3, back_hook), 0)
-    back_full(0, False)
+    lax.fori_loop(0, 2, layers(3, back_hook), 0)
     sync(1)
     finish(1)
 

time: 81.9 us -> 81.9 us (level)
  no operation moved by 1% of the time
where the time goes in v11:
time: 81.9 us; the launch traced here: 81.8 us
  Pallas kernels  80.9 us (99%)
  between operations  0.82 us (1%)
    pallas_call x1, Pallas kernels, device_fn(): pl.pallas_call(main_body, out_shape=shapes + [jax.ShapeDtypeStruct((4, 8,...  72.4 us
    pallas_call x1, Pallas kernels, device_fn(): pl.pallas_call(write_body, out_shape=shapes, in_specs=[VMEM] * 7, out_spe...  8.53 us

profile of v11, /device:TPU:0, one launch (start us, length us, event | category | flops | bytes accessed | tf_op | source)
XLA Modules:
  0.0 81.8 jit_solution(7208226689501749175)
XLA Ops:
  0.6 72.4 %diloco_round.1 = (f32[1,4,256,1024]{3,2,1,0:T(8,128)S(1)}, f32[1,4,1024,256]{3,2,1,0:T(8,128)S(1)}, f32[4,256,1024]{2,1,0:T(8,128)S(1)}, f32[4,1024,256]{2,1,0:...) custom-call(f32[1,4,256,1024]{3,2,1,0:T(8,128)} %w1_in.1, ...), custom_call_target="tpu_custom_call" | custom-call | tf_op jit(solution)/shard_map/diloco_round/pallas_call | solution.py:473
  73.0 8.5 %write_out.1 = (f32[1,4,256,1024]{3,2,1,0:T(8,128)}, f32[1,4,1024,256]{3,2,1,0:T(8,128)}, f32[4,256,1024]{2,1,0:T(8,128)}, f32[4,1024,256]{2,1,0:T(8,128)}, f32[...) custom-call(f32[1,4,256,1024]{3,2,1,0:T(8,128)S(1)} %get-tuple-element.13.w1, f32[1,4,1024,256]{3,2,1,0:T(8,128)S(1)} %get-tuple-element.14.w2, ...), custom_call_target="tpu_custom_call" | custom-call | tf_op jit(solution)/shard_map/write_out/pallas_call | solution.py:493

commit v12 on v11

--- a/solution.py
+++ b/solution.py
@@ -17,6 +17,8 @@
 NB = FF // D
 INNER_LR = 2.0 * D / (FF * L)
 N_ALL = 16
+GELU_K0 = 0.7978845608028654
+GELU_K1 = GELU_K0 * 0.044715
 F32 = jnp.float32
 BF16 = jnp.bfloat16
 MESH = pl.DeviceIdType.MESH
@@ -39,15 +41,14 @@
     return lax.dot_general(a, b, (((ca,), (cb,)), ((), ())), preferred_element_type=F32)
 
 
-def gelu_pair(a):
-    k0 = 0.7978845608028654
-    k1 = k0 * 0.044715
+def gelu_parts(a):
     a2 = a * a
-    t = jnp.tanh(a * (k0 + k1 * a2))
-    h = 0.5 + 0.5 * t
-    u = a * h
-    du = h + (u * (1.0 - h)) * (2.0 * k0 + (6.0 * k1) * a2)
-    return u, du
+    t = jnp.tanh(a * (GELU_K0 + GELU_K1 * a2))
+    return 0.5 + 0.5 * t, a2
+
+
+def gelu_grad(u, h, a2):
+    return h + (u * (1.0 - h)) * (2.0 * GELU_K0 + (6.0 * GELU_K1) * a2)
 
 
 def unit_slice(mat, u):
@@ -173,6 +174,14 @@
             src_ref=src, dst_ref=dst, send_sem=st_send.at[stage, gi], recv_sem=st_recv.at[stage, gi],
             device_id=dev, device_id_type=MESH)
 
+    def keeps_pre_act(k, lay):
+        return k == 2 or (k == 0 and lay < 2)
+
+    def grad_from_pre_act(lay, cols):
+        a = du[lay, :, cols]
+        h, a2 = gelu_parts(a)
+        return gelu_grad(a * h, h, a2)
+
     def forward(k, before_layer_1=None):
         hid[...] = xb[k].astype(F32)
 
@@ -191,10 +200,11 @@
                     w1b[lay, :, cols] = w1[0, lay, :, cols].astype(BF16)
                     w2b[lay, cols, :] = w2[0, lay, cols, :].astype(BF16)
                 a = dot(h_bf, w1b[lay, :, cols], 1, 0)
-                u, dg = gelu_pair(a)
+                h, a2 = gelu_parts(a)
+                u = a * h
                 u_bf = u.astype(BF16)
                 ub[lay, :, cols] = u_bf
-                du[lay, :, cols] = dg
+                du[lay, :, cols] = a if keeps_pre_act(k, lay) else gelu_grad(u, h, a2)
                 acc = acc + dot(u_bf, w2b[lay, cols, :], 1, 0)
             hid[...] = acc
             return 0
@@ -243,7 +253,7 @@
         for j in range(NB):
             cols = slice(j * D, (j + 1) * D)
             d_u = dot(e, w2b[lay, cols, :], 1, 1)
-            c = (du[lay, :, cols] * d_u).astype(BF16)
+            c = (grad_from_pre_act(lay, cols) * d_u).astype(BF16)
             acc = acc + dot(c, w1b[lay, :, cols], 1, 1)
             new1 = w1[0, lay, :, cols] - INNER_LR * dot(h_bf, c, 0, 0)
             w1[0, lay, :, cols] = new1
@@ -255,14 +265,15 @@
         send_piece(i, 1)
         w2b[lay] = w2[0, lay].astype(BF16)
 
-    def back_full(lay, need_input_grad=True):
+    def back_full(lay, need_input_grad=True, pre_act=False):
         e = dhid[...].astype(BF16)
         h_bf = hb[lay]
         acc = dhid[...]
         for j in range(NB):
             cols = slice(j * D, (j + 1) * D)
             d_u = dot(e, w2b[lay, cols, :], 1, 1)
-            c = (du[lay, :, cols] * d_u).astype(BF16)
+            grad = grad_from_pre_act(lay, cols) if pre_act else du[lay, :, cols]
+            c = (grad * d_u).astype(BF16)
             update2(lay, cols, ub[lay, :, cols], e)
             if need_input_grad:
                 acc = acc + dot(c, w1b[lay, :, cols], 1, 1)
@@ -420,8 +431,8 @@
 
     lax.fori_loop(0, 2, layers(3, lambda i, lay: back_send(
         i, lay, lambda: outer_update(last_piece, merge=False))), 0)
-    back_full(1)
-    back_full(0, False)
+    back_full(1, True, True)
+    back_full(0, False, True)
 
     forward(3)
     loss_grad(3)

time: 81.9 us -> 81.5 us (level)
  no operation moved by 1% of the time
where the time goes in v12:
time: 81.5 us; the launch traced here: 81.4 us
  Pallas kernels  80.6 us (99%)
  between operations  0.82 us (1%)
    pallas_call x1, Pallas kernels, device_fn(): pl.pallas_call(main_body, out_shape=shapes + [jax.ShapeDtypeStruct((4, 8,...  72.1 us
    pallas_call x1, Pallas kernels, device_fn(): pl.pallas_call(write_body, out_shape=shapes, in_specs=[VMEM] * 7, out_spe...  8.53 us

profile of v12, /device:TPU:0, one launch (start us, length us, event | category | flops | bytes accessed | tf_op | source)
XLA Modules:
  0.0 81.4 jit_solution(11051324392840230086)
XLA Ops:
  0.6 72.1 %diloco_round.1 = (f32[1,4,256,1024]{3,2,1,0:T(8,128)S(1)}, f32[1,4,1024,256]{3,2,1,0:T(8,128)S(1)}, f32[4,256,1024]{2,1,0:T(8,128)S(1)}, f32[4,1024,256]{2,1,0:...) custom-call(f32[1,4,256,1024]{3,2,1,0:T(8,128)} %w1_in.1, ...), custom_call_target="tpu_custom_call" | custom-call | tf_op jit(solution)/shard_map/diloco_round/pallas_call | solution.py:484
  72.7 8.5 %write_out.1 = (f32[1,4,256,1024]{3,2,1,0:T(8,128)}, f32[1,4,1024,256]{3,2,1,0:T(8,128)}, f32[4,256,1024]{2,1,0:T(8,128)}, f32[4,1024,256]{2,1,0:T(8,128)}, f32[...) custom-call(f32[1,4,256,1024]{3,2,1,0:T(8,128)S(1)} %get-tuple-element.13.w1, f32[1,4,1024,256]{3,2,1,0:T(8,128)S(1)} %get-tuple-element.14.w2, ...), custom_call_target="tpu_custom_call" | custom-call | tf_op jit(solution)/shard_map/write_out/pallas_call | solution.py:504

commit v13 on v12

--- a/solution.py
+++ b/solution.py
@@ -95,8 +95,8 @@
                 pltpu.make_async_copy(w2_in.at[0, lay], w2.at[0, lay], ld_sem.at[L + lay]))
 
     def w_start(lay):
-        for i in range(4):
-            for src, dst, n, idx in ((w1_in, w1, D // 4, lay), (w2_in, w2, FF // 4, L + lay)):
+        for src, dst, n, idx in ((w1_in, w1, D // 4, lay), (w2_in, w2, FF // 4, L + lay)):
+            for i in range(4):
                 rows = pl.ds(i * n, n)
                 pltpu.make_async_copy(src.at[0, lay, rows], dst.at[0, lay, rows], ld_sem.at[idx]).start()
 
@@ -187,8 +187,10 @@
 
         def layer(lay, _):
             if k == 0:
-                for cp in w_load(lay):
-                    cp.wait()
+                load_1, load_2 = w_load(lay)
+                load_1.wait()
+                if lay > 0:
+                    load_2.wait()
             if before_layer_1 is not None and lay == 1:
                 before_layer_1()
             h_bf = hid[...].astype(BF16)
@@ -198,13 +200,16 @@
                 cols = slice(j * D, (j + 1) * D)
                 if k == 0:
                     w1b[lay, :, cols] = w1[0, lay, :, cols].astype(BF16)
-                    w2b[lay, cols, :] = w2[0, lay, cols, :].astype(BF16)
                 a = dot(h_bf, w1b[lay, :, cols], 1, 0)
                 h, a2 = gelu_parts(a)
                 u = a * h
                 u_bf = u.astype(BF16)
                 ub[lay, :, cols] = u_bf
                 du[lay, :, cols] = a if keeps_pre_act(k, lay) else gelu_grad(u, h, a2)
+                if k == 0:
+                    if lay == 0 and j == 0:
+                        load_2.wait()
+                    w2b[lay, cols, :] = w2[0, lay, cols, :].astype(BF16)
                 acc = acc + dot(u_bf, w2b[lay, cols, :], 1, 0)
             hid[...] = acc
             return 0

time: 81.5 us -> 81.5 us (level)
  no operation moved by 1% of the time
where the time goes in v13:
time: 81.5 us; the launch traced here: 81.4 us
  Pallas kernels  80.6 us (99%)
  between operations  0.82 us (1%)
    pallas_call x1, Pallas kernels, device_fn(): pl.pallas_call(main_body, out_shape=shapes + [jax.ShapeDtypeStruct((4, 8,...  72.1 us
    pallas_call x1, Pallas kernels, device_fn(): pl.pallas_call(write_body, out_shape=shapes, in_specs=[VMEM] * 7, out_spe...  8.53 us

profile of v13, /device:TPU:0, one launch (start us, length us, event | category | flops | bytes accessed | tf_op | source)
XLA Modules:
  0.0 81.4 jit_solution(12838857629951750199)
XLA Ops:
  0.6 72.1 %diloco_round.1 = (f32[1,4,256,1024]{3,2,1,0:T(8,128)S(1)}, f32[1,4,1024,256]{3,2,1,0:T(8,128)S(1)}, f32[4,256,1024]{2,1,0:T(8,128)S(1)}, f32[4,1024,256]{2,1,0:...) custom-call(f32[1,4,256,1024]{3,2,1,0:T(8,128)} %w1_in.1, ...), custom_call_target="tpu_custom_call" | custom-call | tf_op jit(solution)/shard_map/diloco_round/pallas_call | solution.py:489
  72.7 8.5 %write_out.1 = (f32[1,4,256,1024]{3,2,1,0:T(8,128)}, f32[1,4,1024,256]{3,2,1,0:T(8,128)}, f32[4,256,1024]{2,1,0:T(8,128)}, f32[4,1024,256]{2,1,0:T(8,128)}, f32[...) custom-call(f32[1,4,256,1024]{3,2,1,0:T(8,128)S(1)} %get-tuple-element.13.w1, f32[1,4,1024,256]{3,2,1,0:T(8,128)S(1)} %get-tuple-element.14.w2, ...), custom_call_target="tpu_custom_call" | custom-call | tf_op jit(solution)/shard_map/write_out/pallas_call | solution.py:509
